TPU v7x, 32 devices: a whole 2x2x4 slice. The times are simulated.
32 devices in a mesh: dp: 8 (over z, x), mp: 4 (over y, core).
Axes of the slice: x: 2, y: 2, z: 4, core: 2. Of those that a mesh axis runs over, the one named last changes fastest.
Arguments:
- images: bfloat16 [4096, 768], P(('dp', 'mp')), may hold values from -64 to 64
- texts: bfloat16 [4096, 768], P(('dp', 'mp')), may hold values from -64 to 64
- log_scale: float32 [1], replicated, may hold values from 2.5 to 3.5
- bias: float32 [1], replicated, may hold values from -6 to -3
Outputs:
- row_loss: float32 [4096], P(('dp', 'mp'))
- col_loss: float32 [4096], P(('dp', 'mp'))
All inputs are finite; a program needn't handle non-finite values.
Results may differ from a plain program's by a relative error of at most 0.0008.
Values may be sent and summed in bfloat16 or wider, within the bound.
No kernel may reach another device: no remote copies, remote signals or barrier semaphores. Data moves between devices by JAX's collectives and lax.ppermute only.
A program may use at most 64 MiB of HBM per device.

v0:
```python
import jax
import jax.numpy as jnp
from jax import lax
from jax.sharding import PartitionSpec as P

TOK_DEV = 512


EPSILON = 1e-06


def unit_rows(values):
    widened = values.astype(jnp.float32)
    inverse = lax.rsqrt(jnp.sum(widened * widened, axis=1, keepdims=True) + EPSILON)
    return (widened * inverse).astype(jnp.bfloat16)


def local(images, texts, log_scale, bias):
    groups = lax.axis_size("mp")
    cycle_size = lax.axis_size("dp")
    myself = lax.axis_index("dp")
    member = lax.axis_index("mp")
    quarter_rows = images.shape[0]
    pair_rows = quarter_rows * groups
    logit_scale = jnp.exp(log_scale[0])
    offset = bias[0]
    staying = lax.all_gather(images, "mp", axis=0, tiled=True)
    fixed_unit = unit_rows(staying)
    travel = unit_rows(texts)
    fixed_ids = lax.broadcasted_iota(jnp.int32, (pair_rows, 1), 0) + myself * pair_rows
    arrived = lax.all_gather(travel, "dp", axis=0, tiled=True)
    scores = lax.dot_general(
        fixed_unit, arrived, (((1,), (1,)), ((), ())), preferred_element_type=jnp.float32
    )
    logits = logit_scale * scores + offset
    gathered = lax.broadcasted_iota(jnp.int32, (1, arrived.shape[0]), 1)
    moving_ids = (
        gathered // quarter_rows * pair_rows + member * quarter_rows + gathered % quarter_rows
    )
    losses = jax.nn.softplus(jnp.where(fixed_ids == moving_ids, -logits, logits))
    stay_total = jnp.sum(losses, axis=1)
    col_table = jnp.sum(losses, axis=0)
    stay_total, col_table = (stay_total, col_table)
    stay_part = lax.psum_scatter(stay_total, "mp", scatter_dimension=0, tiled=True)
    cycle_part = lax.psum_scatter(
        col_table.reshape(cycle_size, quarter_rows), "dp", scatter_dimension=0, tiled=True
    ).reshape(quarter_rows)
    row_sums, col_sums = (stay_part, cycle_part)
    return (row_sums / TOK_DEV, col_sums / TOK_DEV)


def solution(mesh):
    placed = (P(("dp", "mp"), None), P(("dp", "mp"), None), P(), P())
    return jax.shard_map(
        local,
        mesh=mesh,
        in_specs=placed,
        out_specs=(P(("dp", "mp")), P(("dp", "mp"))),
        check_vma=False,
    )
```

profile of v0, /device:TPU:0, one launch (start us, length us, event | category | flops | bytes accessed | tf_op | source)
XLA Modules:
  0.0 94.3 jit_solution(5937984547054298363)
XLA Ops:
  7.2 0.0 all-gather.2.cloned.1.call-start
  7.2 1.0 %fusion.4 = f32[128]{0:T(128)S(1)} fusion(bf16[128,768]{1,0:T(8,128)(2,1)} %param.5), kind=kLoop, calls=%fused_computation.9 | loop fusion | flops 294784 | bytes 197120 | tf_op jit(solution)/shard_map/reduce_sum | solution.py:14
  8.3 1.7 %fusion.5 = bf16[128,768]{1,0:T(8,128)(2,1)} fusion(bf16[128,768]{1,0:T(8,128)(2,1)} %param.5, f32[128]{0:T(128)S(1)} %add_rsqrt_fusion.1), kind=kLoop, calls=%fused_computation.10 | loop fusion | flops 294912 | bytes 393728 | tf_op jit(solution)/shard_map/convert_element_type | solution.py:15
  10.0 0.0 all-gather.2.cloned.1.call-update
  11.3 1.3 %dynamic-slice = u32[1]{0:T(128)} dynamic-slice(u32[32]{0:T(128)} %constant.56, u32[]{:T(128)S(6)} %add.97), dynamic_slice_sizes={1} | dynamic-slice | bytes 12
  12.6 1.3 %dynamic-slice.2 = u32[1]{0:T(128)} dynamic-slice(u32[32]{0:T(128)} %constant.60, u32[]{:T(128)S(6)} %add.97), dynamic_slice_sizes={1} | dynamic-slice | bytes 12
  14.5 10.3 %all_gather.6 = bf16[512,768]{1,0:T(8,128)(2,1)S(1)} all-gather(bf16[128,768]{1,0:T(8,128)(2,1)} %param.4), channel_id=1, replica_groups=mesh['dp'=8,'mp'=4] {'mp'}, dimensions={0}, use_global_device_ids=true | all-gather | bytes 983040 | tf_op jit(solution)/shard_map/all_gather | solution.py:27
  24.8 0.2 fusion
  25.1 32.0 %all-gather.2.cloned.1.call-done = bf16[1024,768]{1,0:T(8,128)(2,1)} async-done(((bf16[128,768]{1,0:T(8,128)(2,1)}), bf16[1024,768]{1,0:T(8,128)(2,1)}) %all-gather.2.cloned.1.call-update) | async-done | bytes 1572880 | tf_op jit(solution)/shard_map/all_gather | solution.py:31
  57.1 3.8 %fusion.17 = (f32[1024]{0:T(1024)S(1)}, f32[512]{0:T(512)S(1)}) fusion(f32[]{:T(128)} %bitcast.8, bf16[1024,768]{1,0:T(8,128)(2,1)} %all-gather.2.cloned.1.call-done, bf16[512,768]{1,0:T(8,128)(2,1)S(1)} %all_gather.6, f32[512]{0:T(512)S(1)} %add_rsqrt_fusion, f32[]{:T(128)} %bitcast, s32[1024]{0:T(1024)S(1)} %fusion.14, s32[512]{0:T(512)S(1)} %iota_add_fusion), kind=kOutput, calls=%fused_computation.31 | convolution fusion | flops 813300224 | bytes 2373640 | tf_op jit(solution)/shard_map/dot_general | solution.py:32
  60.9 5.7 %all-reduce = f32[512]{0:T(512)S(1)} all-reduce(f32[512]{0:T(512)S(1)} %get-tuple-element.3), channel_id=2, replica_groups=mesh['dp'=8,'mp'=4] {'mp'}, use_global_device_ids=true, to_apply=%region_3.4.clone | all-reduce | flops 512 | bytes 4096
  66.5 19.2 %all-reduce.1 = f32[8,128]{1,0:T(8,128)S(1)} all-reduce(f32[8,128]{1,0:T(8,128)S(1)} %bitcast.9), channel_id=3, replica_groups=mesh['dp'=8,'mp'=4] {'dp'}, use_global_device_ids=true, to_apply=%region_5.6.clone | all-reduce | flops 1024 | bytes 8192
  85.7 0.6 dynamic-slice_multiply_fusion.1
  86.3 1.1 %fusion.16 = f32[128]{0:T(128)} fusion(f32[8,128]{1,0:T(8,128)S(1)} %all-reduce.1, u32[]{:T(128)} %bitcast.5), kind=kLoop, calls=%fused_computation.28 | loop fusion | flops 128 | bytes 1028 | tf_op jit(solution)/shard_map/div | solution.py:49
  (4 shorter events, 0.0 us)
Async XLA Ops:
  7.2 49.9 %all-gather.2.cloned.1.call-start = ((), (), s32[]{:S(2)}) async-start(), calls=%async_computation | async-start | bytes 1769472 | tf_op jit(solution)/shard_map/all_gather | solution.py:31
Sparse Core Ops, SparseCore 0:
  10.2 46.8 all-gather.1
where the time goes:
time: 94.6 us; the launch traced here: 94.3 us
  blocking collectives  35.1 us (37%)
  waiting for transfers between devices  32 us (34%)
  between operations  16 us (17%)
  other arithmetic  4.74 us (5%)
  matrix products  3.78 us (4%)
  local copies, waits for them, and re-layouts  2.54 us (3%)
    all_gather x1, waiting for transfers between devices, local(): arrived = lax.all_gather(travel, 'dp', axis=0, tiled=True)  32 us
    unnamed x2, blocking collectives  24.8 us
    all_gather x1, blocking collectives, local(): staying = lax.all_gather(images, 'mp', axis=0, tiled=True)  10.3 us
    dot_general x1, matrix products, local(): lax.dot_general(fixed_unit, arrived, (((1,), (1,)), ((), ())), preferred_...  3.78 us
    unnamed x2, local copies, waits for them, and re-layouts  2.54 us
  transfers between devices with their start and end apart: 1, of which 1 were waited for; matrix products, arithmetic and copies ran while one was open for 3% of the time, Pallas kernels for 0%

commit v1 on v0

v1 whole, which is shorter than its diff:
```python
import math

import jax
import jax.numpy as jnp
from jax import lax
from jax.experimental import pallas as pl
from jax.experimental.pallas import tpu as pltpu
from jax.sharding import PartitionSpec as P

TOK_DEV = 512

EPSILON = 1e-06

AXES = ("dp", "mp")


VMEM = pl.BlockSpec(memory_space=pltpu.VMEM)
SMEM = pl.BlockSpec(memory_space=pltpu.SMEM)


def unit_rows(values):
    widened = values.astype(jnp.float32)
    inverse = lax.rsqrt(jnp.sum(widened * widened, axis=1, keepdims=True) + EPSILON)
    return (widened * inverse).astype(jnp.bfloat16)


def softplus(logits):
    grown = jnp.exp(logits)
    series = grown * (1.0 + grown * (-1.0 / 2 + grown * (1.0 / 3 - grown * (1.0 / 4))))
    return jnp.where(grown < 1.0 / 32, series, jnp.log(1.0 + grown))


def pair_losses(scalars, image_unit, text_unit, own_pairs=False):
    logit_scale, offset = scalars
    scores = lax.dot_general(
        image_unit, text_unit, (((1,), (1,)), ((), ())), preferred_element_type=jnp.float32
    )
    logits = logit_scale * scores + offset
    if own_pairs:
        down = lax.broadcasted_iota(jnp.int32, logits.shape, 0)
        across = lax.broadcasted_iota(jnp.int32, logits.shape, 1)
        logits = jnp.where(down == across, -logits, logits)
    return softplus(logits)


def row_line(losses):
    rows = losses.shape[0]
    lanes = [losses[:, k : k + rows] for k in range(0, losses.shape[1], rows)]
    return jnp.sum(sum(lanes[1:], lanes[0]).T, axis=0, keepdims=True)


def col_tile(losses):
    return jnp.sum(losses.reshape(losses.shape[0] // 8, 8, losses.shape[1]), axis=0)


def col_lines(tile, rows):
    line = jnp.sum(tile, axis=0, keepdims=True)
    return [line[:, k : k + rows] for k in range(0, line.shape[1], rows)]


def own_kernel(log_scale, bias, image, text, scalars, image_unit, text_unit):
    line = scalars.shape[1]
    scalars[0:1, :] = jnp.broadcast_to(jnp.exp(log_scale[...]), (1, line))
    scalars[1:2, :] = jnp.broadcast_to(bias[...], (1, line))
    image_unit[...] = unit_rows(image[...])
    text_unit[...] = unit_rows(text[...])


def loss_scalars(ref):
    return ref[0:1, 0:1], ref[1:2, 0:1]


def early_kernel(n_images, n_texts, scalar_ref, own_image, own_text, *refs):
    images = (own_image,) + refs[: n_images - 1]
    texts = (own_text,) + refs[n_images - 1 : n_images + n_texts - 2]
    row_out, col_out, image_unit, text_unit = refs[n_images + n_texts - 2 :]
    rows = own_image.shape[0]
    scalars = loss_scalars(scalar_ref)
    for j in range(n_texts):
        unit = unit_rows(texts[j][...]) if j else own_text[...]
        text_unit[pl.ds(j * rows, rows), :] = unit
    col_sum = None
    for i in range(n_images):
        unit = unit_rows(images[i][...]) if i else own_image[...]
        image_unit[pl.ds(i * rows, rows), :] = unit
        losses = pair_losses(scalars, unit, text_unit[...], own_pairs=i == 0)
        row_out[i : i + 1, :] = row_line(losses)
        tile = col_tile(losses)
        col_sum = tile if col_sum is None else col_sum + tile
    for j, line in enumerate(col_lines(col_sum, rows)):
        col_out[j : j + 1, :] = line


def late_kernel(n_images, n_texts, core, scalar_ref, *refs):
    early_rows, early_cols, image_unit, text_unit = refs[:4]
    images = refs[4 : 4 + n_images]
    texts = refs[4 + n_images : 4 + n_images + n_texts]
    send, keep, row_total, col_total, late_text = refs[4 + n_images + n_texts :]
    rows = images[0].shape[0]
    n_early_images, n_early_texts = early_rows.shape[0], early_cols.shape[0]
    scalars = loss_scalars(scalar_ref)
    for j in range(n_texts):
        late_text[pl.ds(j * rows, rows), :] = unit_rows(texts[j][...])
    late_sum = None
    for i in range(n_early_images):
        losses = pair_losses(scalars, image_unit[pl.ds(i * rows, rows), :], late_text[...])
        row_total[i : i + 1, :] = early_rows[i : i + 1, :] + row_line(losses)
        tile = col_tile(losses)
        late_sum = tile if late_sum is None else late_sum + tile
    early_sum = None
    for i in range(n_images):
        unit = unit_rows(images[i][...])
        losses = pair_losses(scalars, unit, late_text[...])
        late_sum = late_sum + col_tile(losses)
        line = row_line(losses)
        losses = pair_losses(scalars, unit, text_unit[...])
        tile = col_tile(losses)
        early_sum = tile if early_sum is None else early_sum + tile
        k = n_early_images + i
        row_total[k : k + 1, :] = line + row_line(losses)
    for j, line in enumerate(col_lines(early_sum, rows)):
        col_total[j : j + 1, :] = early_cols[j : j + 1, :] + line
    for j, line in enumerate(col_lines(late_sum, rows)):
        k = n_early_texts + j
        col_total[k : k + 1, :] = line
    send[...] = jnp.zeros_like(send)
    keep[...] = jnp.zeros_like(keep)
    row_units, col_units = row_total.shape[0] // 2, col_total.shape[0]

    @pl.when(core[0] == 0)
    def _():
        for m in range(row_units):
            keep[m] = row_total[2 * m : 2 * m + 2, :] * (1.0 / TOK_DEV)
        for m in range(col_units):
            send[m, 1:2] = col_total[m : m + 1, :] * (1.0 / TOK_DEV)

    @pl.when(core[0] != 0)
    def _():
        for m in range(row_units):
            for k in range(2):
                send[m, k : k + 1] = row_total[2 * m + 1 - k : 2 * m + 2 - k, :] * (1.0 / TOK_DEV)
        for m in range(col_units):
            keep[m, 0:1] = col_total[m : m + 1, :] * (1.0 / TOK_DEV)


def estimate(pairs, width, blocks, rows):
    return pl.CostEstimate(
        flops=2 * pairs * width,
        bytes_accessed=blocks * rows * width * 2,
        transcendentals=2 * pairs,
    )


def own_units(log_scale, bias, image, text):
    unit = jax.ShapeDtypeStruct(image.shape, jnp.bfloat16)
    return pl.pallas_call(
        own_kernel,
        out_shape=(jax.ShapeDtypeStruct((2, 128), jnp.float32), unit, unit),
        in_specs=[VMEM] * 4,
        out_specs=(VMEM,) * 3,
        cost_estimate=pl.CostEstimate(
            flops=8 * image.size, bytes_accessed=8 * image.size, transcendentals=0
        ),
        compiler_params=pltpu.CompilerParams(vmem_limit_bytes=16 << 20),
        name="own_units",
    )(log_scale, bias, image, text)


def early_sums(scalars, own_image, own_text, images, texts):
    rows, width = own_image.shape
    n_images, n_texts = len(images) + 1, len(texts) + 1
    return pl.pallas_call(
        lambda *refs: early_kernel(n_images, n_texts, *refs),
        out_shape=(
            jax.ShapeDtypeStruct((n_images, rows), jnp.float32),
            jax.ShapeDtypeStruct((n_texts, rows), jnp.float32),
            jax.ShapeDtypeStruct((n_images * rows, width), jnp.bfloat16),
            jax.ShapeDtypeStruct((n_texts * rows, width), jnp.bfloat16),
        ),
        in_specs=[VMEM] * (1 + n_images + n_texts),
        out_specs=(VMEM,) * 4,
        cost_estimate=estimate(n_images * n_texts * rows * rows, width, n_images + n_texts, rows),
        compiler_params=pltpu.CompilerParams(vmem_limit_bytes=16 << 20),
        name="early_sums",
    )(scalars, own_image, own_text, *images, *texts)


def late_sums(core, scalars, early, images, texts):
    rows, width = images[0].shape
    n_images, n_texts = len(images), len(texts)
    all_images = early[0].shape[0] + n_images
    all_texts = early[1].shape[0] + n_texts
    pairs = (all_images * all_texts - early[0].shape[0] * early[1].shape[0]) * rows * rows
    units = max(all_images // 2, all_texts)
    return pl.pallas_call(
        lambda *refs: late_kernel(n_images, n_texts, *refs),
        out_shape=(jax.ShapeDtypeStruct((units, 2, rows), jnp.float32),) * 2,
        in_specs=[SMEM] + [VMEM] * (5 + n_images + n_texts),
        out_specs=(VMEM, VMEM),
        scratch_shapes=[
            pltpu.VMEM((all_images, rows), jnp.float32),
            pltpu.VMEM((all_texts, rows), jnp.float32),
            pltpu.VMEM((n_texts * rows, width), jnp.bfloat16),
        ],
        cost_estimate=estimate(pairs, width, all_images + all_texts, rows),
        compiler_params=pltpu.CompilerParams(vmem_limit_bytes=16 << 20),
        name="late_sums",
    )(core, scalars, *early, *images, *texts)


def solution(mesh):
    n_devices = mesh.shape["dp"] * mesh.shape["mp"]
    bits = [1 << k for k in range(int(math.log2(n_devices)))]
    dp_bits = [b for b in bits if b >= mesh.shape["mp"]]
    split = dp_bits[0::2] + dp_bits[1::2]
    text_bits = sorted(split[: len(bits) // 2], reverse=True)
    image_bits = sorted(set(bits) - set(text_bits), reverse=True)
    core_bit, link_bits = image_bits[-1], image_bits[:-1]

    def masks_of(order):
        masks = [0]
        for bit in order:
            masks = masks + [mask | bit for mask in masks]
        return masks

    image_masks = sorted(masks_of(link_bits), key=lambda m: m.bit_count())
    text_masks = sorted(masks_of(text_bits), key=lambda m: m.bit_count())

    def move(value, partner):
        pairs = [(d, partner(d)) for d in range(n_devices) if partner(d) != d]
        return lax.ppermute(value, AXES, pairs)

    def swap(value, bit):
        return move(value, lambda d: d ^ bit)

    def gather(own, order):
        blocks = {0: own}
        for bit in order:
            for mask, block in list(blocks.items()):
                blocks[mask | bit] = swap(block, bit)
        return blocks

    def losses(images, texts, log_scale, bias):
        scalars, own_image, own_text = own_units(
            log_scale.reshape(1, 1), bias.reshape(1, 1), images, texts
        )
        core = (lax.axis_index("mp") & 1).astype(jnp.int32)
        image_blocks = gather(images, link_bits)
        text_blocks = gather(texts, text_bits)
        paired = {m: swap(b, core_bit) for m, b in image_blocks.items()}
        early_masks = [m for m in image_masks if m.bit_count() < 2]
        late_masks = [m for m in image_masks if m.bit_count() >= 2]
        both = lambda masks: [b for m in masks for b in (image_blocks[m], paired[m])]
        early_texts = [text_blocks[m] for m in text_masks if m.bit_count() < 2]
        late_texts = [text_blocks[m] for m in text_masks if m.bit_count() >= 2]
        early = early_sums(
            scalars, own_image, own_text, both(early_masks)[1:], early_texts[1:]
        )
        send, keep = late_sums(
            core.reshape(1), scalars, early, both(late_masks), late_texts
        )
        merged = keep + swap(send, core_bit)
        total = merged[0]
        for k in reversed(range(1, merged.shape[0])):
            row_mask = image_masks[k] if k < len(image_masks) else 0
            col_mask = text_masks[k] if k < len(text_masks) else 0
            total = total + move(merged[k], lambda d: d ^ (col_mask if d & core_bit else row_mask))
        other = swap(total[1:2], core_bit)
        on_rows = core == 0
        own = total[0:1]
        row_loss = jnp.where(on_rows, own, other).reshape(-1)
        col_loss = jnp.where(on_rows, other, own).reshape(-1)
        return row_loss, col_loss

    placed = (P(AXES, None), P(AXES, None), P(), P())
    return jax.shard_map(
        losses,
        mesh=mesh,
        in_specs=placed,
        out_specs=(P(AXES), P(AXES)),
        check_vma=False,
    )
```

time: 94.6 us -> 34 us (0.36)
  blocking collectives: 35.1 us -> 0 us
  waiting for transfers between devices: 32 us -> 8.9 us
  starting transfers between devices: 0.04 us -> 17.5 us
  between operations: 16 us -> 2.02 us
  other arithmetic: 4.74 us -> 0.53 us
  matrix products: 3.78 us -> 0 us
  Pallas kernels: 0 us -> 3.06 us
    all_gather x1 -> x0, waiting for transfers between devices: 32 us -> none  [local(): arrived = lax.all_gather(travel, 'dp', axis=0, tiled=True)]
    unnamed x2 -> x0, blocking collectives: 24.8 us -> none
    ppermute x0 -> x15, starting transfers between devices: none -> 17.5 us  [move(): return lax.ppermute(value, AXES, pairs)]
    all_gather x1 -> x0, blocking collectives: 10.3 us -> none  [local(): staying = lax.all_gather(images, 'mp', axis=0, tiled=True)]
    ppermute x0 -> x15, waiting for transfers between devices: none -> 8.9 us  [move(): return lax.ppermute(value, AXES, pairs)]
    dot_general x1 -> x0, matrix products: 3.78 us -> none  [local(): lax.dot_general(fixed_unit, arrived, (((1,), (1,)), ((), ())), preferred_...]
    pallas_call x0 -> x3, Pallas kernels: none -> 3.06 us  [the longest x1 1.65 us: early_sums(): pl.pallas_call(lambda *refs: early_kernel(n_images, n_texts, *refs), out_...]
    div x2 -> x0, other arithmetic: 1.73 us -> none  [local(): return (row_sums / TOK_DEV, col_sums / TOK_DEV)]
  transfers between devices with their start and end apart: 1 -> 15, of which waited for: 1 -> 7; matrix products, arithmetic and copies ran while one was open for 3% -> 0% of each run, Pallas kernels for 0% -> 5%
where the time goes in v1:
time: 34 us; the launch traced here: 33.9 us
  starting transfers between devices  17.5 us (51%)
  waiting for transfers between devices  8.9 us (26%)
  Pallas kernels  3.06 us (9%)
  between operations  2.02 us (6%)
  local copies, waits for them, and re-layouts  1.86 us (5%)
  other arithmetic  0.53 us (2%)
    ppermute x15, starting transfers between devices, move(): return lax.ppermute(value, AXES, pairs)  17.5 us
    ppermute x15, waiting for transfers between devices, move(): return lax.ppermute(value, AXES, pairs)  8.9 us
    unnamed x4, local copies, waits for them, and re-layouts  1.85 us
    pallas_call x1, Pallas kernels, early_sums(): pl.pallas_call(lambda *refs: early_kernel(n_images, n_texts, *refs), out_...  1.65 us
    pallas_call x1, Pallas kernels, late_sums(): pl.pallas_call(lambda *refs: late_kernel(n_images, n_texts, *refs), out_s...  1.24 us
  transfers between devices with their start and end apart: 15, of which 7 were waited for; matrix products, arithmetic and copies ran while one was open for 0% of the time, Pallas kernels for 5%

profile of v1, /device:TPU:0, one launch (start us, length us, event | category | flops | bytes accessed | tf_op | source)
XLA Modules:
  0.0 33.9 jit_solution(15138914762449720442)
XLA Ops:
  0.6 3.1 %collective-permute-start.1 = (bf16[128,768]{1,0:T(8,128)(2,1)}, bf16[128,768]{1,0:T(8,128)(2,1)S(1)}, u32[]{:S(2)}, u32[]{:S(2)}) collective-permute-start(bf16[128,768]{1,0:T(8,128)(2,1)} %image.1), channel_id=1, source_target_pairs={{0,8},{1,9},{2,10},{3,11},{4,12},{5,13},{6,14},{7,15},{8,0},{9,1},... | collective-permute-start | bytes 589832 | tf_op jit(solution)/shard_map/ppermute | solution.py:231
  3.7 1.5 %collective-permute-start.3 = (bf16[128,768]{1,0:T(8,128)(2,1)}, bf16[128,768]{1,0:T(8,128)(2,1)S(1)}, u32[]{:S(2)}, u32[]{:S(2)}) collective-permute-start(bf16[128,768]{1,0:T(8,128)(2,1)} %image.1), channel_id=1, source_target_pairs={{0,2},{1,3},{2,0},{3,1},{4,6},{5,7},{6,4},{7,5},{8,10},{9,11},{10,... | collective-permute-start | bytes 589832 | tf_op jit(solution)/shard_map/ppermute | solution.py:231
  5.3 2.6 %collective-permute-start.5 = (bf16[128,768]{1,0:T(8,128)(2,1)}, bf16[128,768]{1,0:T(8,128)(2,1)S(1)}, u32[]{:S(2)}, u32[]{:S(2)}) collective-permute-start(bf16[128,768]{1,0:T(8,128)(2,1)} %text.1), channel_id=1, source_target_pairs={{0,16},{1,17},{2,18},{3,19},{4,20},{5,21},{6,22},{7,23},{8,24},{9,... | collective-permute-start | bytes 589832 | tf_op jit(solution)/shard_map/ppermute | solution.py:231
  7.9 0.0 collective-permute-start
  7.9 3.2 %collective-permute-done.1.refs_4_ = bf16[128,768]{1,0:T(8,128)(2,1)S(1)} collective-permute-done((bf16[128,768]{1,0:T(8,128)(2,1)}, bf16[128,768]{1,0:T(8,128)(2,1)S(1)}, u32[]{:S(2)}, u32[]{:S(2)}) %collective-permute-start.1) | collective-permute-done | bytes 196640 | tf_op jit(solution)/shard_map/ppermute | solution.py:231
  11.0 3.4 %collective-permute-start.7 = (bf16[128,768]{1,0:T(8,128)(2,1)S(1)}, bf16[128,768]{1,0:T(8,128)(2,1)S(1)}, u32[]{:S(2)}, u32[]{:S(2)}) collective-permute-start(bf16[128,768]{1,0:T(8,128)(2,1)S(1)} %collective-permute-done.1.refs_4_), channel_id=1, source_target_pairs={{0,2},{1,3},{2,0},{3,1},{4,6},{5,7},{6,4},{7,5},{8,10},{9,11},{10,... | collective-permute-start | bytes 589832 | tf_op jit(solution)/shard_map/ppermute | solution.py:231
  14.4 1.5 %collective-permute-start.6 = (bf16[128,768]{1,0:T(8,128)(2,1)}, bf16[128,768]{1,0:T(8,128)(2,1)S(1)}, u32[]{:S(2)}, u32[]{:S(2)}) collective-permute-start(bf16[128,768]{1,0:T(8,128)(2,1)} %text.1), channel_id=1, source_target_pairs={{0,4},{1,5},{2,6},{3,7},{4,0},{5,1},{6,2},{7,3},{8,12},{9,13},{10,... | collective-permute-start | bytes 589832 | tf_op jit(solution)/shard_map/ppermute | solution.py:231
  15.9 0.0 collective-permute-done.3.refs_6_
  15.9 0.0 collective-permute-start.2
  15.9 0.8 %collective-permute-done.5.refs_8_ = bf16[128,768]{1,0:T(8,128)(2,1)S(1)} collective-permute-done((bf16[128,768]{1,0:T(8,128)(2,1)}, bf16[128,768]{1,0:T(8,128)(2,1)S(1)}, u32[]{:S(2)}, u32[]{:S(2)}) %collective-permute-start.5) | collective-permute-done | bytes 196640 | tf_op jit(solution)/shard_map/ppermute | solution.py:231
  16.7 0.0 collective-permute-start.4
  16.7 0.0 collective-permute-done.refs_3_
  16.7 1.5 %collective-permute-start.9 = (bf16[128,768]{1,0:T(8,128)(2,1)S(1)}, bf16[128,768]{1,0:T(8,128)(2,1)S(1)}, u32[]{:S(2)}, u32[]{:S(2)}) collective-permute-start(bf16[128,768]{1,0:T(8,128)(2,1)S(1)} %collective-permute-done.5.refs_8_), channel_id=1, source_target_pairs={{0,4},{1,5},{2,6},{3,7},{4,0},{5,1},{6,2},{7,3},{8,12},{9,13},{10,... | collective-permute-start | bytes 589832 | tf_op jit(solution)/shard_map/ppermute | solution.py:231
  18.2 0.2 collective-permute-start.8
  19.8 0.9 %copy-done = bf16[128,768]{1,0:T(8,128)(2,1)S(1)} copy-done((bf16[128,768]{1,0:T(8,128)(2,1)S(1)}, bf16[128,768]{1,0:T(8,128)(2,1)}, u32[]{:S(2)}) %copy-start) | copy-done | bytes 196632
  20.7 0.9 %copy-done.1 = bf16[128,768]{1,0:T(8,128)(2,1)S(1)} copy-done((bf16[128,768]{1,0:T(8,128)(2,1)S(1)}, bf16[128,768]{1,0:T(8,128)(2,1)}, u32[]{:S(2)}) %copy-start.1) | copy-done | bytes 196632
  21.6 0.2 own_units.1
  21.8 0.0 collective-permute-done.6.refs_9_
  21.8 0.0 collective-permute-done.4.refs_7_
  21.8 1.6 %early_sums.1 = (f32[6,128]{1,0:T(8,128)S(1)}, f32[3,128]{1,0:T(4,128)S(1)}, bf16[768,768]{1,0:T(8,128)(2,1)S(1)}, bf16[384,768]{1,0:T(8,128)(2,1)S(1)}) custom-call(f32[2,128]{1,0:T(2,128)S(1)} %get-tuple-element.11.refs_0_.refs_1_, bf16[128,768]{1,0:T(8,128)(2,1)S(1)} %get-tuple-element.12.refs_1_, bf16[128,768]{1,0:T(8,128)(2,1)S(1)} %get-tuple-element.13.refs_2_, ...), custom_call_target="tpu_custom_call" | custom-call | flops 452984832 | bytes 1769472 | tf_op jit(solution)/shard_map/early_sums/pallas_call | solution.py:172
  23.5 1.0 %collective-permute-done.9.refs_8_ = bf16[128,768]{1,0:T(8,128)(2,1)S(1)} collective-permute-done((bf16[128,768]{1,0:T(8,128)(2,1)S(1)}, bf16[128,768]{1,0:T(8,128)(2,1)S(1)}, u32[]{:S(2)}, u32[]{:S(2)}) %collective-permute-start.9) | collective-permute-done | bytes 196640 | tf_op jit(solution)/shard_map/ppermute | solution.py:231
  24.5 1.2 %late_sums.1 = (f32[4,2,128]{2,1,0:T(2,128)S(1)}, f32[4,2,128]{2,1,0:T(2,128)S(1)}) custom-call(s32[1]{0:T(128)} %bitcast.refs_0_, f32[2,128]{1,0:T(2,128)S(1)} %get-tuple-element.11.refs_0_.refs_1_, f32[6,128]{1,0:T(8,128)S(1)} %get-tuple-element.14.refs_2_, f32[3,128]{1,0:T(4,128)S(1)} %get-tuple-element.15.refs_3_, ...), custom_call_target="tpu_custom_call" | custom-call | flops 352321536 | bytes 2359296 | tf_op jit(solution)/shard_map/late_sums/pallas_call | solution.py:195
  25.8 0.1 collective-permute-start.10
  25.8 1.2 %collective-permute-done.10 = f32[4,2,128]{2,1,0:T(2,128)S(1)} collective-permute-done((f32[4,2,128]{2,1,0:T(2,128)S(1)}, f32[4,2,128]{2,1,0:T(2,128)S(1)}, u32[]{:S(2)}, u32[]{:S(2)}) %collective-permute-start.10) | collective-permute-done | bytes 4128 | tf_op jit(solution)/shard_map/ppermute | solution.py:231
  27.0 0.1 collective-permute-start.11
  27.1 1.1 %collective-permute-start.12 = (f32[2,128]{1,0:T(2,128)S(1)}, f32[2,128]{1,0:T(2,128)S(1)}, u32[]{:S(2)}, u32[]{:S(2)}) collective-permute-start(f32[2,128]{1,0:T(2,128)S(1)} %get-tuple-element.22), channel_id=1, source_target_pairs={{0,2},{1,5},{2,0},{3,7},{4,6},{5,1},{6,4},{7,3},{8,10},{9,13},{10,... | collective-permute-start | bytes 3080 | tf_op jit(solution)/shard_map/ppermute | solution.py:231
  28.2 2.3 %collective-permute-start.13 = (f32[2,128]{1,0:T(2,128)S(1)}, f32[2,128]{1,0:T(2,128)S(1)}, u32[]{:S(2)}, u32[]{:S(2)}) collective-permute-start(f32[2,128]{1,0:T(2,128)S(1)} %get-tuple-element.21), channel_id=1, source_target_pairs={{0,8},{1,17},{2,10},{3,19},{4,12},{5,21},{6,14},{7,23},{8,0},{9,25... | collective-permute-start | bytes 3080 | tf_op jit(solution)/shard_map/ppermute | solution.py:231
  30.5 1.0 %collective-permute-done.11 = f32[2,128]{1,0:T(2,128)S(1)} collective-permute-done((f32[2,128]{1,0:T(2,128)S(1)}, f32[2,128]{1,0:T(2,128)S(1)}, u32[]{:S(2)}, u32[]{:S(2)}) %collective-permute-start.11) | collective-permute-done | bytes 1056 | tf_op jit(solution)/shard_map/ppermute | solution.py:231
  31.5 0.6 %collective-permute-done.13 = f32[2,128]{1,0:T(2,128)S(1)} collective-permute-done((f32[2,128]{1,0:T(2,128)S(1)}, f32[2,128]{1,0:T(2,128)S(1)}, u32[]{:S(2)}, u32[]{:S(2)}) %collective-permute-start.13) | collective-permute-done | bytes 1056 | tf_op jit(solution)/shard_map/ppermute | solution.py:231
  32.1 0.1 collective-permute-start.14
  32.2 1.1 %collective-permute-done.14 = f32[1,128]{1,0:T(1,128)S(1)} collective-permute-done((f32[1,128]{1,0:T(1,128)S(1)}, f32[1,128]{1,0:T(1,128)S(1)}, u32[]{:S(2)}, u32[]{:S(2)}) %collective-permute-start.14) | collective-permute-done | bytes 544 | tf_op jit(solution)/shard_map/ppermute | solution.py:231
  33.3 0.5 %fusion.4 = (f32[128]{0:T(128)}, f32[128]{0:T(128)}) fusion(f32[1,128]{1,0:T(1,128)S(1)} %collective-permute-done.14, pred[]{:T(512)S(6)} %eq.3, f32[2,128]{1,0:T(2,128)S(1)} %fusion.2), kind=kLoop, calls=%fused_computation.10 | loop fusion | flops 256 | bytes 2049 | tf_op jit(solution)/shard_map/reshape | solution.py:272
  (10 shorter events, 0.0 us)
Async XLA Ops:
  0.6 10.4 %collective-permute-start.1 = (bf16[128,768]{1,0:T(8,128)(2,1)}, bf16[128,768]{1,0:T(8,128)(2,1)S(1)}, u32[]{:S(2)}, u32[]{:S(2)}) collective-permute-start(bf16[128,768]{1,0:T(8,128)(2,1)} %image.1), channel_id=1, source_target_pairs={{0,8},{1,9},{2,10},{3,11},{4,12},{5,13},{6,14},{7,15},{8,0},{9,1},... | collective-permute-start | bytes 589832 | tf_op jit(solution)/shard_map/ppermute | solution.py:231
  3.7 12.2 %collective-permute-start.3 = (bf16[128,768]{1,0:T(8,128)(2,1)}, bf16[128,768]{1,0:T(8,128)(2,1)S(1)}, u32[]{:S(2)}, u32[]{:S(2)}) collective-permute-start(bf16[128,768]{1,0:T(8,128)(2,1)} %image.1), channel_id=1, source_target_pairs={{0,2},{1,3},{2,0},{3,1},{4,6},{5,7},{6,4},{7,5},{8,10},{9,11},{10,... | collective-permute-start | bytes 589832 | tf_op jit(solution)/shard_map/ppermute | solution.py:231
  5.3 11.5 %collective-permute-start.5 = (bf16[128,768]{1,0:T(8,128)(2,1)}, bf16[128,768]{1,0:T(8,128)(2,1)S(1)}, u32[]{:S(2)}, u32[]{:S(2)}) collective-permute-start(bf16[128,768]{1,0:T(8,128)(2,1)} %text.1), channel_id=1, source_target_pairs={{0,16},{1,17},{2,18},{3,19},{4,20},{5,21},{6,22},{7,23},{8,24},{9,... | collective-permute-start | bytes 589832 | tf_op jit(solution)/shard_map/ppermute | solution.py:231
  7.9 8.9 %collective-permute-start = (bf16[128,768]{1,0:T(8,128)(2,1)}, bf16[128,768]{1,0:T(8,128)(2,1)S(1)}, u32[]{:S(2)}, u32[]{:S(2)}) collective-permute-start(bf16[128,768]{1,0:T(8,128)(2,1)} %image.1), channel_id=1, source_target_pairs={{0,1},{1,0},{2,3},{3,2},{4,5},{5,4},{6,7},{7,6},{8,9},{9,8},{10,11... | collective-permute-start | bytes 589832 | tf_op jit(solution)/shard_map/ppermute | solution.py:231
  11.0 7.2 %collective-permute-start.7 = (bf16[128,768]{1,0:T(8,128)(2,1)S(1)}, bf16[128,768]{1,0:T(8,128)(2,1)S(1)}, u32[]{:S(2)}, u32[]{:S(2)}) collective-permute-start(bf16[128,768]{1,0:T(8,128)(2,1)S(1)} %collective-permute-done.1.refs_4_), channel_id=1, source_target_pairs={{0,2},{1,3},{2,0},{3,1},{4,6},{5,7},{6,4},{7,5},{8,10},{9,11},{10,... | collective-permute-start | bytes 589832 | tf_op jit(solution)/shard_map/ppermute | solution.py:231
  14.4 7.4 %collective-permute-start.6 = (bf16[128,768]{1,0:T(8,128)(2,1)}, bf16[128,768]{1,0:T(8,128)(2,1)S(1)}, u32[]{:S(2)}, u32[]{:S(2)}) collective-permute-start(bf16[128,768]{1,0:T(8,128)(2,1)} %text.1), channel_id=1, source_target_pairs={{0,4},{1,5},{2,6},{3,7},{4,0},{5,1},{6,2},{7,3},{8,12},{9,13},{10,... | collective-permute-start | bytes 589832 | tf_op jit(solution)/shard_map/ppermute | solution.py:231
  15.9 5.9 %collective-permute-start.2 = (bf16[128,768]{1,0:T(8,128)(2,1)S(1)}, bf16[128,768]{1,0:T(8,128)(2,1)S(1)}, u32[]{:S(2)}, u32[]{:S(2)}) collective-permute-start(bf16[128,768]{1,0:T(8,128)(2,1)S(1)} %collective-permute-done.1.refs_4_), channel_id=1, source_target_pairs={{0,1},{1,0},{2,3},{3,2},{4,5},{5,4},{6,7},{7,6},{8,9},{9,8},{10,11... | collective-permute-start | bytes 589832 | tf_op jit(solution)/shard_map/ppermute | solution.py:231
  16.7 5.1 %collective-permute-start.4 = (bf16[128,768]{1,0:T(8,128)(2,1)S(1)}, bf16[128,768]{1,0:T(8,128)(2,1)S(1)}, u32[]{:S(2)}, u32[]{:S(2)}) collective-permute-start(bf16[128,768]{1,0:T(8,128)(2,1)S(1)} %collective-permute-done.3.refs_6_), channel_id=1, source_target_pairs={{0,1},{1,0},{2,3},{3,2},{4,5},{5,4},{6,7},{7,6},{8,9},{9,8},{10,11... | collective-permute-start | bytes 589832 | tf_op jit(solution)/shard_map/ppermute | solution.py:231
  16.7 7.8 %collective-permute-start.9 = (bf16[128,768]{1,0:T(8,128)(2,1)S(1)}, bf16[128,768]{1,0:T(8,128)(2,1)S(1)}, u32[]{:S(2)}, u32[]{:S(2)}) collective-permute-start(bf16[128,768]{1,0:T(8,128)(2,1)S(1)} %collective-permute-done.5.refs_8_), channel_id=1, source_target_pairs={{0,4},{1,5},{2,6},{3,7},{4,0},{5,1},{6,2},{7,3},{8,12},{9,13},{10,... | collective-permute-start | bytes 589832 | tf_op jit(solution)/shard_map/ppermute | solution.py:231
  18.2 6.3 %collective-permute-start.8 = (bf16[128,768]{1,0:T(8,128)(2,1)S(1)}, bf16[128,768]{1,0:T(8,128)(2,1)S(1)}, u32[]{:S(2)}, u32[]{:S(2)}) collective-permute-start(bf16[128,768]{1,0:T(8,128)(2,1)S(1)} %collective-permute-done.7.refs_6_), channel_id=1, source_target_pairs={{0,1},{1,0},{2,3},{3,2},{4,5},{5,4},{6,7},{7,6},{8,9},{9,8},{10,11... | collective-permute-start | bytes 589832 | tf_op jit(solution)/shard_map/ppermute | solution.py:231
  19.7 0.9 %copy-start = (bf16[128,768]{1,0:T(8,128)(2,1)S(1)}, bf16[128,768]{1,0:T(8,128)(2,1)}, u32[]{:S(2)}) copy-start(bf16[128,768]{1,0:T(8,128)(2,1)} %image.1) | copy-start | bytes 589828
  20.7 0.9 %copy-start.1 = (bf16[128,768]{1,0:T(8,128)(2,1)S(1)}, bf16[128,768]{1,0:T(8,128)(2,1)}, u32[]{:S(2)}) copy-start(bf16[128,768]{1,0:T(8,128)(2,1)} %text.1) | copy-start | bytes 589828
  25.8 1.2 %collective-permute-start.10 = (f32[4,2,128]{2,1,0:T(2,128)S(1)}, f32[4,2,128]{2,1,0:T(2,128)S(1)}, u32[]{:S(2)}, u32[]{:S(2)}) collective-permute-start(f32[4,2,128]{2,1,0:T(2,128)S(1)} %get-tuple-element.19), channel_id=1, source_target_pairs={{0,1},{1,0},{2,3},{3,2},{4,5},{5,4},{6,7},{7,6},{8,9},{9,8},{10,11... | collective-permute-start | bytes 12296 | tf_op jit(solution)/shard_map/ppermute | solution.py:231
  27.0 4.5 %collective-permute-start.11 = (f32[2,128]{1,0:T(2,128)S(1)}, f32[2,128]{1,0:T(2,128)S(1)}, u32[]{:S(2)}, u32[]{:S(2)}) collective-permute-start(f32[2,128]{1,0:T(2,128)S(1)} %get-tuple-element.20), channel_id=1, source_target_pairs={{0,10},{1,21},{2,8},{3,23},{4,14},{5,17},{6,12},{7,19},{8,2},{9,29... | collective-permute-start | bytes 3080 | tf_op jit(solution)/shard_map/ppermute | solution.py:231
  27.1 4.5 %collective-permute-start.12 = (f32[2,128]{1,0:T(2,128)S(1)}, f32[2,128]{1,0:T(2,128)S(1)}, u32[]{:S(2)}, u32[]{:S(2)}) collective-permute-start(f32[2,128]{1,0:T(2,128)S(1)} %get-tuple-element.22), channel_id=1, source_target_pairs={{0,2},{1,5},{2,0},{3,7},{4,6},{5,1},{6,4},{7,3},{8,10},{9,13},{10,... | collective-permute-start | bytes 3080 | tf_op jit(solution)/shard_map/ppermute | solution.py:231
  28.2 3.9 %collective-permute-start.13 = (f32[2,128]{1,0:T(2,128)S(1)}, f32[2,128]{1,0:T(2,128)S(1)}, u32[]{:S(2)}, u32[]{:S(2)}) collective-permute-start(f32[2,128]{1,0:T(2,128)S(1)} %get-tuple-element.21), channel_id=1, source_target_pairs={{0,8},{1,17},{2,10},{3,19},{4,12},{5,21},{6,14},{7,23},{8,0},{9,25... | collective-permute-start | bytes 3080 | tf_op jit(solution)/shard_map/ppermute | solution.py:231
  32.1 1.2 %collective-permute-start.14 = (f32[1,128]{1,0:T(1,128)S(1)}, f32[1,128]{1,0:T(1,128)S(1)}, u32[]{:S(2)}, u32[]{:S(2)}) collective-permute-start(f32[1,128]{1,0:T(1,128)S(1)} %slice.23), channel_id=1, source_target_pairs={{0,1},{1,0},{2,3},{3,2},{4,5},{5,4},{6,7},{7,6},{8,9},{9,8},{10,11... | collective-permute-start | bytes 1544 | tf_op jit(solution)/shard_map/ppermute | solution.py:231

commit v2 on v1

--- a/solution.py
+++ b/solution.py
@@ -245,7 +245,8 @@
             log_scale.reshape(1, 1), bias.reshape(1, 1), images, texts
         )
         core = (lax.axis_index("mp") & 1).astype(jnp.int32)
-        image_blocks = gather(images, link_bits)
+        image_blocks = {m: move(images, lambda d: d ^ m) for m in image_masks if m}
+        image_blocks[0] = images
         text_blocks = gather(texts, text_bits)
         paired = {m: swap(b, core_bit) for m, b in image_blocks.items()}
         early_masks = [m for m in image_masks if m.bit_count() < 2]
@@ -261,7 +262,7 @@
         )
         merged = keep + swap(send, core_bit)
         total = merged[0]
-        for k in reversed(range(1, merged.shape[0])):
+        for k in range(1, merged.shape[0]):
             row_mask = image_masks[k] if k < len(image_masks) else 0
             col_mask = text_masks[k] if k < len(text_masks) else 0
             total = total + move(merged[k], lambda d: d ^ (col_mask if d & core_bit else row_mask))

time: 34 us -> 37.8 us (1.11)
  waiting for transfers between devices: 8.9 us -> 14 us
  starting transfers between devices: 17.5 us -> 16.1 us
    ppermute x15, waiting for transfers between devices: 8.9 us -> 14 us  [move(): return lax.ppermute(value, AXES, pairs)]
    ppermute x15, starting transfers between devices: 17.5 us -> 16.1 us  [move(): return lax.ppermute(value, AXES, pairs)]
  transfers between devices with their start and end apart: 15 -> 15, of which waited for: 7 -> 9; matrix products, arithmetic and copies ran while one was open for 0% -> 0% of each run, Pallas kernels for 5% -> 5%
where the time goes in v2:
time: 37.8 us; the launch traced here: 37.6 us
  starting transfers between devices  16.1 us (43%)
  waiting for transfers between devices  14 us (37%)
  Pallas kernels  3.06 us (8%)
  between operations  2.01 us (5%)
  local copies, waits for them, and re-layouts  1.86 us (5%)
  other arithmetic  0.53 us (1%)
    ppermute x15, starting transfers between devices, move(): return lax.ppermute(value, AXES, pairs)  16.1 us
    ppermute x15, waiting for transfers between devices, move(): return lax.ppermute(value, AXES, pairs)  14 us
    unnamed x4, local copies, waits for them, and re-layouts  1.85 us
    pallas_call x1, Pallas kernels, early_sums(): pl.pallas_call(lambda *refs: early_kernel(n_images, n_texts, *refs), out_...  1.64 us
    pallas_call x1, Pallas kernels, late_sums(): pl.pallas_call(lambda *refs: late_kernel(n_images, n_texts, *refs), out_s...  1.24 us
  transfers between devices with their start and end apart: 15, of which 9 were waited for; matrix products, arithmetic and copies ran while one was open for 0% of the time, Pallas kernels for 5%

profile of v2, /device:TPU:0, one launch (start us, length us, event | category | flops | bytes accessed | tf_op | source)
XLA Modules:
  0.0 37.6 jit_solution(10900701275508212488)
XLA Ops:
  0.6 3.1 %collective-permute-start.1 = (bf16[128,768]{1,0:T(8,128)(2,1)}, bf16[128,768]{1,0:T(8,128)(2,1)S(1)}, u32[]{:S(2)}, u32[]{:S(2)}) collective-permute-start(bf16[128,768]{1,0:T(8,128)(2,1)} %image.1), channel_id=1, source_target_pairs={{0,8},{1,9},{2,10},{3,11},{4,12},{5,13},{6,14},{7,15},{8,0},{9,1},... | collective-permute-start | bytes 589832 | tf_op jit(solution)/shard_map/ppermute | solution.py:231
  3.7 1.5 %collective-permute-start.3 = (bf16[128,768]{1,0:T(8,128)(2,1)}, bf16[128,768]{1,0:T(8,128)(2,1)S(1)}, u32[]{:S(2)}, u32[]{:S(2)}) collective-permute-start(bf16[128,768]{1,0:T(8,128)(2,1)} %image.1), channel_id=1, source_target_pairs={{0,2},{1,3},{2,0},{3,1},{4,6},{5,7},{6,4},{7,5},{8,10},{9,11},{10,... | collective-permute-start | bytes 589832 | tf_op jit(solution)/shard_map/ppermute | solution.py:231
  5.3 2.6 %collective-permute-start.5 = (bf16[128,768]{1,0:T(8,128)(2,1)}, bf16[128,768]{1,0:T(8,128)(2,1)S(1)}, u32[]{:S(2)}, u32[]{:S(2)}) collective-permute-start(bf16[128,768]{1,0:T(8,128)(2,1)} %text.1), channel_id=1, source_target_pairs={{0,16},{1,17},{2,18},{3,19},{4,20},{5,21},{6,22},{7,23},{8,24},{9,... | collective-permute-start | bytes 589832 | tf_op jit(solution)/shard_map/ppermute | solution.py:231
  7.9 0.4 %collective-permute-start.7 = (bf16[128,768]{1,0:T(8,128)(2,1)}, bf16[128,768]{1,0:T(8,128)(2,1)S(1)}, u32[]{:S(2)}, u32[]{:S(2)}) collective-permute-start(bf16[128,768]{1,0:T(8,128)(2,1)} %image.1), channel_id=1, source_target_pairs={{0,10},{1,11},{2,8},{3,9},{4,14},{5,15},{6,12},{7,13},{8,2},{9,3},... | collective-permute-start | bytes 589832 | tf_op jit(solution)/shard_map/ppermute | solution.py:231
  8.2 0.0 collective-permute-start
  8.3 3.8 %collective-permute-done.1.refs_4_ = bf16[128,768]{1,0:T(8,128)(2,1)S(1)} collective-permute-done((bf16[128,768]{1,0:T(8,128)(2,1)}, bf16[128,768]{1,0:T(8,128)(2,1)S(1)}, u32[]{:S(2)}, u32[]{:S(2)}) %collective-permute-start.1) | collective-permute-done | bytes 196640 | tf_op jit(solution)/shard_map/ppermute | solution.py:231
  12.1 2.0 %collective-permute-start.6 = (bf16[128,768]{1,0:T(8,128)(2,1)}, bf16[128,768]{1,0:T(8,128)(2,1)S(1)}, u32[]{:S(2)}, u32[]{:S(2)}) collective-permute-start(bf16[128,768]{1,0:T(8,128)(2,1)} %text.1), channel_id=1, source_target_pairs={{0,4},{1,5},{2,6},{3,7},{4,0},{5,1},{6,2},{7,3},{8,12},{9,13},{10,... | collective-permute-start | bytes 589832 | tf_op jit(solution)/shard_map/ppermute | solution.py:231
  14.0 0.0 collective-permute-done.3.refs_6_
  14.1 0.0 collective-permute-start.2
  14.1 2.8 %collective-permute-done.5.refs_8_ = bf16[128,768]{1,0:T(8,128)(2,1)S(1)} collective-permute-done((bf16[128,768]{1,0:T(8,128)(2,1)}, bf16[128,768]{1,0:T(8,128)(2,1)S(1)}, u32[]{:S(2)}, u32[]{:S(2)}) %collective-permute-start.5) | collective-permute-done | bytes 196640 | tf_op jit(solution)/shard_map/ppermute | solution.py:231
  16.8 0.0 collective-permute-start.4
  16.8 1.6 %collective-permute-done.7.refs_6_ = bf16[128,768]{1,0:T(8,128)(2,1)S(1)} collective-permute-done((bf16[128,768]{1,0:T(8,128)(2,1)}, bf16[128,768]{1,0:T(8,128)(2,1)S(1)}, u32[]{:S(2)}, u32[]{:S(2)}) %collective-permute-start.7) | collective-permute-done | bytes 196640 | tf_op jit(solution)/shard_map/ppermute | solution.py:231
  18.4 1.5 %collective-permute-start.9 = (bf16[128,768]{1,0:T(8,128)(2,1)S(1)}, bf16[128,768]{1,0:T(8,128)(2,1)S(1)}, u32[]{:S(2)}, u32[]{:S(2)}) collective-permute-start(bf16[128,768]{1,0:T(8,128)(2,1)S(1)} %collective-permute-done.5.refs_8_), channel_id=1, source_target_pairs={{0,4},{1,5},{2,6},{3,7},{4,0},{5,1},{6,2},{7,3},{8,12},{9,13},{10,... | collective-permute-start | bytes 589832 | tf_op jit(solution)/shard_map/ppermute | solution.py:231
  21.2 0.9 %copy-done = bf16[128,768]{1,0:T(8,128)(2,1)S(1)} copy-done((bf16[128,768]{1,0:T(8,128)(2,1)S(1)}, bf16[128,768]{1,0:T(8,128)(2,1)}, u32[]{:S(2)}) %copy-start) | copy-done | bytes 196632
  22.1 0.9 %copy-done.1 = bf16[128,768]{1,0:T(8,128)(2,1)S(1)} copy-done((bf16[128,768]{1,0:T(8,128)(2,1)S(1)}, bf16[128,768]{1,0:T(8,128)(2,1)}, u32[]{:S(2)}) %copy-start.1) | copy-done | bytes 196632
  23.1 0.2 own_units.1
  23.2 0.0 collective-permute-done.6.refs_9_
  23.3 0.0 collective-permute-done.2.refs_5_
  23.3 1.6 %early_sums.1 = (f32[6,128]{1,0:T(8,128)S(1)}, f32[3,128]{1,0:T(4,128)S(1)}, bf16[768,768]{1,0:T(8,128)(2,1)S(1)}, bf16[384,768]{1,0:T(8,128)(2,1)S(1)}) custom-call(f32[2,128]{1,0:T(2,128)S(1)} %get-tuple-element.11.refs_0_.refs_1_, bf16[128,768]{1,0:T(8,128)(2,1)S(1)} %get-tuple-element.12.refs_1_, bf16[128,768]{1,0:T(8,128)(2,1)S(1)} %get-tuple-element.13.refs_2_, ...), custom_call_target="tpu_custom_call" | custom-call | flops 452984832 | bytes 1769472 | tf_op jit(solution)/shard_map/early_sums/pallas_call | solution.py:172
  24.9 0.8 %collective-permute-done.9.refs_8_ = bf16[128,768]{1,0:T(8,128)(2,1)S(1)} collective-permute-done((bf16[128,768]{1,0:T(8,128)(2,1)S(1)}, bf16[128,768]{1,0:T(8,128)(2,1)S(1)}, u32[]{:S(2)}, u32[]{:S(2)}) %collective-permute-start.9) | collective-permute-done | bytes 196640 | tf_op jit(solution)/shard_map/ppermute | solution.py:231
  25.7 1.2 %late_sums.1 = (f32[4,2,128]{2,1,0:T(2,128)S(1)}, f32[4,2,128]{2,1,0:T(2,128)S(1)}) custom-call(s32[1]{0:T(128)} %bitcast.refs_0_, f32[2,128]{1,0:T(2,128)S(1)} %get-tuple-element.11.refs_0_.refs_1_, f32[6,128]{1,0:T(8,128)S(1)} %get-tuple-element.14.refs_2_, f32[3,128]{1,0:T(4,128)S(1)} %get-tuple-element.15.refs_3_, ...), custom_call_target="tpu_custom_call" | custom-call | flops 352321536 | bytes 2359296 | tf_op jit(solution)/shard_map/late_sums/pallas_call | solution.py:195
  27.0 0.1 collective-permute-start.10
  27.1 1.2 %collective-permute-done.10 = f32[4,2,128]{2,1,0:T(2,128)S(1)} collective-permute-done((f32[4,2,128]{2,1,0:T(2,128)S(1)}, f32[4,2,128]{2,1,0:T(2,128)S(1)}, u32[]{:S(2)}, u32[]{:S(2)}) %collective-permute-start.10) | collective-permute-done | bytes 4128 | tf_op jit(solution)/shard_map/ppermute | solution.py:231
  28.2 1.7 %collective-permute-start.11 = (f32[2,128]{1,0:T(2,128)S(1)}, f32[2,128]{1,0:T(2,128)S(1)}, u32[]{:S(2)}, u32[]{:S(2)}) collective-permute-start(f32[2,128]{1,0:T(2,128)S(1)} %get-tuple-element.20), channel_id=1, source_target_pairs={{0,8},{1,17},{2,10},{3,19},{4,12},{5,21},{6,14},{7,23},{8,0},{9,25... | collective-permute-start | bytes 3080 | tf_op jit(solution)/shard_map/ppermute | solution.py:231
  29.9 0.5 %collective-permute-start.12 = (f32[2,128]{1,0:T(2,128)S(1)}, f32[2,128]{1,0:T(2,128)S(1)}, u32[]{:S(2)}, u32[]{:S(2)}) collective-permute-start(f32[2,128]{1,0:T(2,128)S(1)} %get-tuple-element.22), channel_id=1, source_target_pairs={{0,2},{1,5},{2,0},{3,7},{4,6},{5,1},{6,4},{7,3},{8,10},{9,13},{10,... | collective-permute-start | bytes 3080 | tf_op jit(solution)/shard_map/ppermute | solution.py:231
  30.4 1.4 %collective-permute-start.13 = (f32[2,128]{1,0:T(2,128)S(1)}, f32[2,128]{1,0:T(2,128)S(1)}, u32[]{:S(2)}, u32[]{:S(2)}) collective-permute-start(f32[2,128]{1,0:T(2,128)S(1)} %get-tuple-element.21), channel_id=1, source_target_pairs={{0,10},{1,21},{2,8},{3,23},{4,14},{5,17},{6,12},{7,19},{8,2},{9,29... | collective-permute-start | bytes 3080 | tf_op jit(solution)/shard_map/ppermute | solution.py:231
  31.8 0.1 collective-permute-done.11
  31.8 1.6 %collective-permute-done.12 = f32[2,128]{1,0:T(2,128)S(1)} collective-permute-done((f32[2,128]{1,0:T(2,128)S(1)}, f32[2,128]{1,0:T(2,128)S(1)}, u32[]{:S(2)}, u32[]{:S(2)}) %collective-permute-start.12) | collective-permute-done | bytes 1056 | tf_op jit(solution)/shard_map/ppermute | solution.py:231
  33.5 1.4 %collective-permute-done.13 = f32[2,128]{1,0:T(2,128)S(1)} collective-permute-done((f32[2,128]{1,0:T(2,128)S(1)}, f32[2,128]{1,0:T(2,128)S(1)}, u32[]{:S(2)}, u32[]{:S(2)}) %collective-permute-start.13) | collective-permute-done | bytes 1056 | tf_op jit(solution)/shard_map/ppermute | solution.py:231
  34.9 1.4 %collective-permute-start.14 = (f32[1,128]{1,0:T(1,128)S(1)}, f32[1,128]{1,0:T(1,128)S(1)}, u32[]{:S(2)}, u32[]{:S(2)}) collective-permute-start(f32[1,128]{1,0:T(1,128)S(1)} %slice.23), channel_id=1, source_target_pairs={{0,1},{1,0},{2,3},{3,2},{4,5},{5,4},{6,7},{7,6},{8,9},{9,8},{10,11... | collective-permute-start | bytes 1544 | tf_op jit(solution)/shard_map/ppermute | solution.py:231
  36.2 0.8 %collective-permute-done.14 = f32[1,128]{1,0:T(1,128)S(1)} collective-permute-done((f32[1,128]{1,0:T(1,128)S(1)}, f32[1,128]{1,0:T(1,128)S(1)}, u32[]{:S(2)}, u32[]{:S(2)}) %collective-permute-start.14) | collective-permute-done | bytes 544 | tf_op jit(solution)/shard_map/ppermute | solution.py:231
  37.1 0.5 %fusion.4 = (f32[128]{0:T(128)}, f32[128]{0:T(128)}) fusion(f32[1,128]{1,0:T(1,128)S(1)} %collective-permute-done.14, pred[]{:T(512)S(6)} %eq.3, f32[2,128]{1,0:T(2,128)S(1)} %fusion.2), kind=kLoop, calls=%fused_computation.10 | loop fusion | flops 256 | bytes 2049 | tf_op jit(solution)/shard_map/reshape | solution.py:273
  (10 shorter events, 0.0 us)
Async XLA Ops:
  0.6 11.4 %collective-permute-start.1 = (bf16[128,768]{1,0:T(8,128)(2,1)}, bf16[128,768]{1,0:T(8,128)(2,1)S(1)}, u32[]{:S(2)}, u32[]{:S(2)}) collective-permute-start(bf16[128,768]{1,0:T(8,128)(2,1)} %image.1), channel_id=1, source_target_pairs={{0,8},{1,9},{2,10},{3,11},{4,12},{5,13},{6,14},{7,15},{8,0},{9,1},... | collective-permute-start | bytes 589832 | tf_op jit(solution)/shard_map/ppermute | solution.py:231
  3.7 10.3 %collective-permute-start.3 = (bf16[128,768]{1,0:T(8,128)(2,1)}, bf16[128,768]{1,0:T(8,128)(2,1)S(1)}, u32[]{:S(2)}, u32[]{:S(2)}) collective-permute-start(bf16[128,768]{1,0:T(8,128)(2,1)} %image.1), channel_id=1, source_target_pairs={{0,2},{1,3},{2,0},{3,1},{4,6},{5,7},{6,4},{7,5},{8,10},{9,11},{10,... | collective-permute-start | bytes 589832 | tf_op jit(solution)/shard_map/ppermute | solution.py:231
  5.3 11.6 %collective-permute-start.5 = (bf16[128,768]{1,0:T(8,128)(2,1)}, bf16[128,768]{1,0:T(8,128)(2,1)S(1)}, u32[]{:S(2)}, u32[]{:S(2)}) collective-permute-start(bf16[128,768]{1,0:T(8,128)(2,1)} %text.1), channel_id=1, source_target_pairs={{0,16},{1,17},{2,18},{3,19},{4,20},{5,21},{6,22},{7,23},{8,24},{9,... | collective-permute-start | bytes 589832 | tf_op jit(solution)/shard_map/ppermute | solution.py:231
  7.9 10.5 %collective-permute-start.7 = (bf16[128,768]{1,0:T(8,128)(2,1)}, bf16[128,768]{1,0:T(8,128)(2,1)S(1)}, u32[]{:S(2)}, u32[]{:S(2)}) collective-permute-start(bf16[128,768]{1,0:T(8,128)(2,1)} %image.1), channel_id=1, source_target_pairs={{0,10},{1,11},{2,8},{3,9},{4,14},{5,15},{6,12},{7,13},{8,2},{9,3},... | collective-permute-start | bytes 589832 | tf_op jit(solution)/shard_map/ppermute | solution.py:231
  8.2 10.2 %collective-permute-start = (bf16[128,768]{1,0:T(8,128)(2,1)}, bf16[128,768]{1,0:T(8,128)(2,1)S(1)}, u32[]{:S(2)}, u32[]{:S(2)}) collective-permute-start(bf16[128,768]{1,0:T(8,128)(2,1)} %image.1), channel_id=1, source_target_pairs={{0,1},{1,0},{2,3},{3,2},{4,5},{5,4},{6,7},{7,6},{8,9},{9,8},{10,11... | collective-permute-start | bytes 589832 | tf_op jit(solution)/shard_map/ppermute | solution.py:231
  12.1 11.2 %collective-permute-start.6 = (bf16[128,768]{1,0:T(8,128)(2,1)}, bf16[128,768]{1,0:T(8,128)(2,1)S(1)}, u32[]{:S(2)}, u32[]{:S(2)}) collective-permute-start(bf16[128,768]{1,0:T(8,128)(2,1)} %text.1), channel_id=1, source_target_pairs={{0,4},{1,5},{2,6},{3,7},{4,0},{5,1},{6,2},{7,3},{8,12},{9,13},{10,... | collective-permute-start | bytes 589832 | tf_op jit(solution)/shard_map/ppermute | solution.py:231
  14.1 9.2 %collective-permute-start.2 = (bf16[128,768]{1,0:T(8,128)(2,1)S(1)}, bf16[128,768]{1,0:T(8,128)(2,1)S(1)}, u32[]{:S(2)}, u32[]{:S(2)}) collective-permute-start(bf16[128,768]{1,0:T(8,128)(2,1)S(1)} %collective-permute-done.1.refs_4_), channel_id=1, source_target_pairs={{0,1},{1,0},{2,3},{3,2},{4,5},{5,4},{6,7},{7,6},{8,9},{9,8},{10,11... | collective-permute-start | bytes 589832 | tf_op jit(solution)/shard_map/ppermute | solution.py:231
  16.8 6.5 %collective-permute-start.4 = (bf16[128,768]{1,0:T(8,128)(2,1)S(1)}, bf16[128,768]{1,0:T(8,128)(2,1)S(1)}, u32[]{:S(2)}, u32[]{:S(2)}) collective-permute-start(bf16[128,768]{1,0:T(8,128)(2,1)S(1)} %collective-permute-done.3.refs_6_), channel_id=1, source_target_pairs={{0,1},{1,0},{2,3},{3,2},{4,5},{5,4},{6,7},{7,6},{8,9},{9,8},{10,11... | collective-permute-start | bytes 589832 | tf_op jit(solution)/shard_map/ppermute | solution.py:231
  18.4 6.5 %collective-permute-start.8 = (bf16[128,768]{1,0:T(8,128)(2,1)S(1)}, bf16[128,768]{1,0:T(8,128)(2,1)S(1)}, u32[]{:S(2)}, u32[]{:S(2)}) collective-permute-start(bf16[128,768]{1,0:T(8,128)(2,1)S(1)} %collective-permute-done.7.refs_6_), channel_id=1, source_target_pairs={{0,1},{1,0},{2,3},{3,2},{4,5},{5,4},{6,7},{7,6},{8,9},{9,8},{10,11... | collective-permute-start | bytes 589832 | tf_op jit(solution)/shard_map/ppermute | solution.py:231
  18.4 7.3 %collective-permute-start.9 = (bf16[128,768]{1,0:T(8,128)(2,1)S(1)}, bf16[128,768]{1,0:T(8,128)(2,1)S(1)}, u32[]{:S(2)}, u32[]{:S(2)}) collective-permute-start(bf16[128,768]{1,0:T(8,128)(2,1)S(1)} %collective-permute-done.5.refs_8_), channel_id=1, source_target_pairs={{0,4},{1,5},{2,6},{3,7},{4,0},{5,1},{6,2},{7,3},{8,12},{9,13},{10,... | collective-permute-start | bytes 589832 | tf_op jit(solution)/shard_map/ppermute | solution.py:231
  21.2 0.9 %copy-start = (bf16[128,768]{1,0:T(8,128)(2,1)S(1)}, bf16[128,768]{1,0:T(8,128)(2,1)}, u32[]{:S(2)}) copy-start(bf16[128,768]{1,0:T(8,128)(2,1)} %image.1) | copy-start | bytes 589828
  22.1 0.9 %copy-start.1 = (bf16[128,768]{1,0:T(8,128)(2,1)S(1)}, bf16[128,768]{1,0:T(8,128)(2,1)}, u32[]{:S(2)}) copy-start(bf16[128,768]{1,0:T(8,128)(2,1)} %text.1) | copy-start | bytes 589828
  27.0 1.2 %collective-permute-start.10 = (f32[4,2,128]{2,1,0:T(2,128)S(1)}, f32[4,2,128]{2,1,0:T(2,128)S(1)}, u32[]{:S(2)}, u32[]{:S(2)}) collective-permute-start(f32[4,2,128]{2,1,0:T(2,128)S(1)} %get-tuple-element.19), channel_id=1, source_target_pairs={{0,1},{1,0},{2,3},{3,2},{4,5},{5,4},{6,7},{7,6},{8,9},{9,8},{10,11... | collective-permute-start | bytes 12296 | tf_op jit(solution)/shard_map/ppermute | solution.py:231
  28.2 3.6 %collective-permute-start.11 = (f32[2,128]{1,0:T(2,128)S(1)}, f32[2,128]{1,0:T(2,128)S(1)}, u32[]{:S(2)}, u32[]{:S(2)}) collective-permute-start(f32[2,128]{1,0:T(2,128)S(1)} %get-tuple-element.20), channel_id=1, source_target_pairs={{0,8},{1,17},{2,10},{3,19},{4,12},{5,21},{6,14},{7,23},{8,0},{9,25... | collective-permute-start | bytes 3080 | tf_op jit(solution)/shard_map/ppermute | solution.py:231
  29.9 3.6 %collective-permute-start.12 = (f32[2,128]{1,0:T(2,128)S(1)}, f32[2,128]{1,0:T(2,128)S(1)}, u32[]{:S(2)}, u32[]{:S(2)}) collective-permute-start(f32[2,128]{1,0:T(2,128)S(1)} %get-tuple-element.22), channel_id=1, source_target_pairs={{0,2},{1,5},{2,0},{3,7},{4,6},{5,1},{6,4},{7,3},{8,10},{9,13},{10,... | collective-permute-start | bytes 3080 | tf_op jit(solution)/shard_map/ppermute | solution.py:231
  30.4 4.5 %collective-permute-start.13 = (f32[2,128]{1,0:T(2,128)S(1)}, f32[2,128]{1,0:T(2,128)S(1)}, u32[]{:S(2)}, u32[]{:S(2)}) collective-permute-start(f32[2,128]{1,0:T(2,128)S(1)} %get-tuple-element.21), channel_id=1, source_target_pairs={{0,10},{1,21},{2,8},{3,23},{4,14},{5,17},{6,12},{7,19},{8,2},{9,29... | collective-permute-start | bytes 3080 | tf_op jit(solution)/shard_map/ppermute | solution.py:231
  34.9 2.2 %collective-permute-start.14 = (f32[1,128]{1,0:T(1,128)S(1)}, f32[1,128]{1,0:T(1,128)S(1)}, u32[]{:S(2)}, u32[]{:S(2)}) collective-permute-start(f32[1,128]{1,0:T(1,128)S(1)} %slice.23), channel_id=1, source_target_pairs={{0,1},{1,0},{2,3},{3,2},{4,5},{5,4},{6,7},{7,6},{8,9},{9,8},{10,11... | collective-permute-start | bytes 1544 | tf_op jit(solution)/shard_map/ppermute | solution.py:231

commit v3 on v2

--- a/solution.py
+++ b/solution.py
@@ -11,6 +11,8 @@
 
 EPSILON = 1e-06
 
+LOG2_E = math.log2(math.e)
+
 AXES = ("dp", "mp")
 
 
@@ -24,10 +26,9 @@
     return (widened * inverse).astype(jnp.bfloat16)
 
 
-def softplus(logits):
-    grown = jnp.exp(logits)
-    series = grown * (1.0 + grown * (-1.0 / 2 + grown * (1.0 / 3 - grown * (1.0 / 4))))
-    return jnp.where(grown < 1.0 / 32, series, jnp.log(1.0 + grown))
+def softplus(grown):
+    series = grown * (1.0 + grown * (-1.0 / 2 + grown * (1.0 / 3)))
+    return jnp.where(grown < 1.0 / 64, series, jnp.log(1.0 + grown))
 
 
 def pair_losses(scalars, image_unit, text_unit, own_pairs=False):
@@ -40,7 +41,7 @@
         down = lax.broadcasted_iota(jnp.int32, logits.shape, 0)
         across = lax.broadcasted_iota(jnp.int32, logits.shape, 1)
         logits = jnp.where(down == across, -logits, logits)
-    return softplus(logits)
+    return softplus(jnp.exp2(logits))
 
 
 def row_line(losses):
@@ -60,8 +61,8 @@
 
 def own_kernel(log_scale, bias, image, text, scalars, image_unit, text_unit):
     line = scalars.shape[1]
-    scalars[0:1, :] = jnp.broadcast_to(jnp.exp(log_scale[...]), (1, line))
-    scalars[1:2, :] = jnp.broadcast_to(bias[...], (1, line))
+    scalars[0:1, :] = jnp.broadcast_to(jnp.exp(log_scale[...]) * LOG2_E, (1, line))
+    scalars[1:2, :] = jnp.broadcast_to(bias[...] * LOG2_E, (1, line))
     image_unit[...] = unit_rows(image[...])
     text_unit[...] = unit_rows(text[...])
 
@@ -95,29 +96,26 @@
     early_rows, early_cols, image_unit, text_unit = refs[:4]
     images = refs[4 : 4 + n_images]
     texts = refs[4 + n_images : 4 + n_images + n_texts]
-    send, keep, row_total, col_total, late_text = refs[4 + n_images + n_texts :]
+    send, keep, row_total, col_total, late_text, late_image = refs[4 + n_images + n_texts :]
     rows = images[0].shape[0]
     n_early_images, n_early_texts = early_rows.shape[0], early_cols.shape[0]
     scalars = loss_scalars(scalar_ref)
     for j in range(n_texts):
         late_text[pl.ds(j * rows, rows), :] = unit_rows(texts[j][...])
-    late_sum = None
+    losses = pair_losses(scalars, image_unit[...], late_text[...])
+    late_sum = col_tile(losses)
     for i in range(n_early_images):
-        losses = pair_losses(scalars, image_unit[pl.ds(i * rows, rows), :], late_text[...])
-        row_total[i : i + 1, :] = early_rows[i : i + 1, :] + row_line(losses)
-        tile = col_tile(losses)
-        late_sum = tile if late_sum is None else late_sum + tile
-    early_sum = None
+        line = row_line(losses[i * rows : i * rows + rows])
+        row_total[i : i + 1, :] = early_rows[i : i + 1, :] + line
     for i in range(n_images):
-        unit = unit_rows(images[i][...])
-        losses = pair_losses(scalars, unit, late_text[...])
-        late_sum = late_sum + col_tile(losses)
-        line = row_line(losses)
-        losses = pair_losses(scalars, unit, text_unit[...])
-        tile = col_tile(losses)
-        early_sum = tile if early_sum is None else early_sum + tile
-        k = n_early_images + i
-        row_total[k : k + 1, :] = line + row_line(losses)
+        late_image[pl.ds(i * rows, rows), :] = unit_rows(images[i][...])
+    losses = pair_losses(scalars, late_image[...], late_text[...])
+    late_sum = late_sum + col_tile(losses)
+    others = pair_losses(scalars, late_image[...], text_unit[...])
+    early_sum = col_tile(others)
+    for i in range(n_images):
+        span, k = slice(i * rows, i * rows + rows), n_early_images + i
+        row_total[k : k + 1, :] = row_line(losses[span]) + row_line(others[span])
     for j, line in enumerate(col_lines(early_sum, rows)):
         col_total[j : j + 1, :] = early_cols[j : j + 1, :] + line
     for j, line in enumerate(col_lines(late_sum, rows)):
@@ -201,6 +199,7 @@
             pltpu.VMEM((all_images, rows), jnp.float32),
             pltpu.VMEM((all_texts, rows), jnp.float32),
             pltpu.VMEM((n_texts * rows, width), jnp.bfloat16),
+            pltpu.VMEM((n_images * rows, width), jnp.bfloat16),
         ],
         cost_estimate=estimate(pairs, width, all_images + all_texts, rows),
         compiler_params=pltpu.CompilerParams(vmem_limit_bytes=16 << 20),
@@ -217,14 +216,17 @@
     image_bits = sorted(set(bits) - set(text_bits), reverse=True)
     core_bit, link_bits = image_bits[-1], image_bits[:-1]
 
+    rank = {0: 0}
+
     def masks_of(order):
         masks = [0]
         for bit in order:
-            masks = masks + [mask | bit for mask in masks]
-        return masks
-
-    image_masks = sorted(masks_of(link_bits), key=lambda m: m.bit_count())
-    text_masks = sorted(masks_of(text_bits), key=lambda m: m.bit_count())
+            rank.update({mask ^ bit: rank[mask] + 1 for mask in masks})
+            masks = masks + [mask ^ bit for mask in masks]
+        return sorted(masks, key=rank.get)
+
+    image_masks = masks_of(link_bits)
+    text_masks = masks_of(text_bits)
 
     def move(value, partner):
         pairs = [(d, partner(d)) for d in range(n_devices) if partner(d) != d]
@@ -237,7 +239,7 @@
         blocks = {0: own}
         for bit in order:
             for mask, block in list(blocks.items()):
-                blocks[mask | bit] = swap(block, bit)
+                blocks[mask ^ bit] = swap(block, bit)
         return blocks
 
     def losses(images, texts, log_scale, bias):
@@ -249,11 +251,11 @@
         image_blocks[0] = images
         text_blocks = gather(texts, text_bits)
         paired = {m: swap(b, core_bit) for m, b in image_blocks.items()}
-        early_masks = [m for m in image_masks if m.bit_count() < 2]
-        late_masks = [m for m in image_masks if m.bit_count() >= 2]
+        early_masks = [m for m in image_masks if rank[m] < 2]
+        late_masks = [m for m in image_masks if rank[m] >= 2]
         both = lambda masks: [b for m in masks for b in (image_blocks[m], paired[m])]
-        early_texts = [text_blocks[m] for m in text_masks if m.bit_count() < 2]
-        late_texts = [text_blocks[m] for m in text_masks if m.bit_count() >= 2]
+        early_texts = [text_blocks[m] for m in text_masks if rank[m] < 2]
+        late_texts = [text_blocks[m] for m in text_masks if rank[m] >= 2]
         early = early_sums(
             scalars, own_image, own_text, both(early_masks)[1:], early_texts[1:]
         )

time: 37.8 us -> 37.6 us (level)
  no operation moved by 1% of the time
where the time goes in v3:
time: 37.6 us; the launch traced here: 37.5 us
  starting transfers between devices  16.1 us (43%)
  waiting for transfers between devices  14.1 us (38%)
  Pallas kernels  2.86 us (8%)
  between operations  2 us (5%)
  local copies, waits for them, and re-layouts  1.86 us (5%)
  other arithmetic  0.53 us (1%)
    ppermute x15, starting transfers between devices, move(): return lax.ppermute(value, AXES, pairs)  16.1 us
    ppermute x15, waiting for transfers between devices, move(): return lax.ppermute(value, AXES, pairs)  14.1 us
    unnamed x4, local copies, waits for them, and re-layouts  1.85 us
    pallas_call x1, Pallas kernels, early_sums(): pl.pallas_call(lambda *refs: early_kernel(n_images, n_texts, *refs), out_...  1.57 us
    pallas_call x1, Pallas kernels, late_sums(): pl.pallas_call(lambda *refs: late_kernel(n_images, n_texts, *refs), out_s...  1.11 us
  transfers between devices with their start and end apart: 15, of which 9 were waited for; matrix products, arithmetic and copies ran while one was open for 0% of the time, Pallas kernels for 5%

profile of v3, /device:TPU:0, one launch (start us, length us, event | category | flops | bytes accessed | tf_op | source)
XLA Modules:
  0.0 37.5 jit_solution(4285671982758873190)
XLA Ops:
  0.6 3.1 %collective-permute-start.1 = (bf16[128,768]{1,0:T(8,128)(2,1)}, bf16[128,768]{1,0:T(8,128)(2,1)S(1)}, u32[]{:S(2)}, u32[]{:S(2)}) collective-permute-start(bf16[128,768]{1,0:T(8,128)(2,1)} %image.1), channel_id=1, source_target_pairs={{0,8},{1,9},{2,10},{3,11},{4,12},{5,13},{6,14},{7,15},{8,0},{9,1},... | collective-permute-start | bytes 589832 | tf_op jit(solution)/shard_map/ppermute | solution.py:233
  3.7 1.5 %collective-permute-start.3 = (bf16[128,768]{1,0:T(8,128)(2,1)}, bf16[128,768]{1,0:T(8,128)(2,1)S(1)}, u32[]{:S(2)}, u32[]{:S(2)}) collective-permute-start(bf16[128,768]{1,0:T(8,128)(2,1)} %image.1), channel_id=1, source_target_pairs={{0,2},{1,3},{2,0},{3,1},{4,6},{5,7},{6,4},{7,5},{8,10},{9,11},{10,... | collective-permute-start | bytes 589832 | tf_op jit(solution)/shard_map/ppermute | solution.py:233
  5.3 2.6 %collective-permute-start.5 = (bf16[128,768]{1,0:T(8,128)(2,1)}, bf16[128,768]{1,0:T(8,128)(2,1)S(1)}, u32[]{:S(2)}, u32[]{:S(2)}) collective-permute-start(bf16[128,768]{1,0:T(8,128)(2,1)} %text.1), channel_id=1, source_target_pairs={{0,16},{1,17},{2,18},{3,19},{4,20},{5,21},{6,22},{7,23},{8,24},{9,... | collective-permute-start | bytes 589832 | tf_op jit(solution)/shard_map/ppermute | solution.py:233
  7.9 0.4 %collective-permute-start.7 = (bf16[128,768]{1,0:T(8,128)(2,1)}, bf16[128,768]{1,0:T(8,128)(2,1)S(1)}, u32[]{:S(2)}, u32[]{:S(2)}) collective-permute-start(bf16[128,768]{1,0:T(8,128)(2,1)} %image.1), channel_id=1, source_target_pairs={{0,10},{1,11},{2,8},{3,9},{4,14},{5,15},{6,12},{7,13},{8,2},{9,3},... | collective-permute-start | bytes 589832 | tf_op jit(solution)/shard_map/ppermute | solution.py:233
  8.2 0.0 collective-permute-start
  8.3 3.8 %collective-permute-done.1.refs_4_ = bf16[128,768]{1,0:T(8,128)(2,1)S(1)} collective-permute-done((bf16[128,768]{1,0:T(8,128)(2,1)}, bf16[128,768]{1,0:T(8,128)(2,1)S(1)}, u32[]{:S(2)}, u32[]{:S(2)}) %collective-permute-start.1) | collective-permute-done | bytes 196640 | tf_op jit(solution)/shard_map/ppermute | solution.py:233
  12.1 2.0 %collective-permute-start.6 = (bf16[128,768]{1,0:T(8,128)(2,1)}, bf16[128,768]{1,0:T(8,128)(2,1)S(1)}, u32[]{:S(2)}, u32[]{:S(2)}) collective-permute-start(bf16[128,768]{1,0:T(8,128)(2,1)} %text.1), channel_id=1, source_target_pairs={{0,4},{1,5},{2,6},{3,7},{4,0},{5,1},{6,2},{7,3},{8,12},{9,13},{10,... | collective-permute-start | bytes 589832 | tf_op jit(solution)/shard_map/ppermute | solution.py:233
  14.0 0.0 collective-permute-done.3.refs_6_
  14.1 0.0 collective-permute-start.2
  14.1 2.8 %collective-permute-done.5.refs_8_ = bf16[128,768]{1,0:T(8,128)(2,1)S(1)} collective-permute-done((bf16[128,768]{1,0:T(8,128)(2,1)}, bf16[128,768]{1,0:T(8,128)(2,1)S(1)}, u32[]{:S(2)}, u32[]{:S(2)}) %collective-permute-start.5) | collective-permute-done | bytes 196640 | tf_op jit(solution)/shard_map/ppermute | solution.py:233
  16.8 1.6 %collective-permute-done.7.refs_6_ = bf16[128,768]{1,0:T(8,128)(2,1)S(1)} collective-permute-done((bf16[128,768]{1,0:T(8,128)(2,1)}, bf16[128,768]{1,0:T(8,128)(2,1)S(1)}, u32[]{:S(2)}, u32[]{:S(2)}) %collective-permute-start.7) | collective-permute-done | bytes 196640 | tf_op jit(solution)/shard_map/ppermute | solution.py:233
  18.4 1.5 %collective-permute-start.9 = (bf16[128,768]{1,0:T(8,128)(2,1)S(1)}, bf16[128,768]{1,0:T(8,128)(2,1)S(1)}, u32[]{:S(2)}, u32[]{:S(2)}) collective-permute-start(bf16[128,768]{1,0:T(8,128)(2,1)S(1)} %collective-permute-done.5.refs_8_), channel_id=1, source_target_pairs={{0,4},{1,5},{2,6},{3,7},{4,0},{5,1},{6,2},{7,3},{8,12},{9,13},{10,... | collective-permute-start | bytes 589832 | tf_op jit(solution)/shard_map/ppermute | solution.py:233
  21.2 0.9 %copy-done = bf16[128,768]{1,0:T(8,128)(2,1)S(1)} copy-done((bf16[128,768]{1,0:T(8,128)(2,1)S(1)}, bf16[128,768]{1,0:T(8,128)(2,1)}, u32[]{:S(2)}) %copy-start) | copy-done | bytes 196632
  22.1 0.9 %copy-done.1 = bf16[128,768]{1,0:T(8,128)(2,1)S(1)} copy-done((bf16[128,768]{1,0:T(8,128)(2,1)S(1)}, bf16[128,768]{1,0:T(8,128)(2,1)}, u32[]{:S(2)}) %copy-start.1) | copy-done | bytes 196632
  23.1 0.2 own_units.1
  23.2 0.0 collective-permute-done.6.refs_9_
  23.3 0.0 collective-permute-done.2.refs_5_
  23.3 1.6 %early_sums.1 = (f32[6,128]{1,0:T(8,128)S(1)}, f32[3,128]{1,0:T(4,128)S(1)}, bf16[768,768]{1,0:T(8,128)(2,1)S(1)}, bf16[384,768]{1,0:T(8,128)(2,1)S(1)}) custom-call(f32[2,128]{1,0:T(2,128)S(1)} %get-tuple-element.11.refs_0_.refs_1_, bf16[128,768]{1,0:T(8,128)(2,1)S(1)} %get-tuple-element.12.refs_1_, bf16[128,768]{1,0:T(8,128)(2,1)S(1)} %get-tuple-element.13.refs_2_, ...), custom_call_target="tpu_custom_call" | custom-call | flops 452984832 | bytes 1769472 | tf_op jit(solution)/shard_map/early_sums/pallas_call | solution.py:170
  24.8 0.0 collective-permute-done.8.refs_7_
  24.9 0.9 %collective-permute-done.9.refs_8_ = bf16[128,768]{1,0:T(8,128)(2,1)S(1)} collective-permute-done((bf16[128,768]{1,0:T(8,128)(2,1)S(1)}, bf16[128,768]{1,0:T(8,128)(2,1)S(1)}, u32[]{:S(2)}, u32[]{:S(2)}) %collective-permute-start.9) | collective-permute-done | bytes 196640 | tf_op jit(solution)/shard_map/ppermute | solution.py:233
  25.7 1.1 %late_sums.1 = (f32[4,2,128]{2,1,0:T(2,128)S(1)}, f32[4,2,128]{2,1,0:T(2,128)S(1)}) custom-call(s32[1]{0:T(128)} %bitcast.refs_0_, f32[2,128]{1,0:T(2,128)S(1)} %get-tuple-element.11.refs_0_.refs_1_, f32[6,128]{1,0:T(8,128)S(1)} %get-tuple-element.14.refs_2_, f32[3,128]{1,0:T(4,128)S(1)} %get-tuple-element.15.refs_3_, ...), custom_call_target="tpu_custom_call" | custom-call | flops 352321536 | bytes 2359296 | tf_op jit(solution)/shard_map/late_sums/pallas_call | solution.py:193
  26.8 0.1 collective-permute-start.10
  26.9 1.2 %collective-permute-done.10 = f32[4,2,128]{2,1,0:T(2,128)S(1)} collective-permute-done((f32[4,2,128]{2,1,0:T(2,128)S(1)}, f32[4,2,128]{2,1,0:T(2,128)S(1)}, u32[]{:S(2)}, u32[]{:S(2)}) %collective-permute-start.10) | collective-permute-done | bytes 4128 | tf_op jit(solution)/shard_map/ppermute | solution.py:233
  28.1 1.7 %collective-permute-start.11 = (f32[2,128]{1,0:T(2,128)S(1)}, f32[2,128]{1,0:T(2,128)S(1)}, u32[]{:S(2)}, u32[]{:S(2)}) collective-permute-start(f32[2,128]{1,0:T(2,128)S(1)} %get-tuple-element.20), channel_id=1, source_target_pairs={{0,8},{1,17},{2,10},{3,19},{4,12},{5,21},{6,14},{7,23},{8,0},{9,25... | collective-permute-start | bytes 3080 | tf_op jit(solution)/shard_map/ppermute | solution.py:233
  29.8 0.5 %collective-permute-start.12 = (f32[2,128]{1,0:T(2,128)S(1)}, f32[2,128]{1,0:T(2,128)S(1)}, u32[]{:S(2)}, u32[]{:S(2)}) collective-permute-start(f32[2,128]{1,0:T(2,128)S(1)} %get-tuple-element.22), channel_id=1, source_target_pairs={{0,2},{1,5},{2,0},{3,7},{4,6},{5,1},{6,4},{7,3},{8,10},{9,13},{10,... | collective-permute-start | bytes 3080 | tf_op jit(solution)/shard_map/ppermute | solution.py:233
  30.3 1.4 %collective-permute-start.13 = (f32[2,128]{1,0:T(2,128)S(1)}, f32[2,128]{1,0:T(2,128)S(1)}, u32[]{:S(2)}, u32[]{:S(2)}) collective-permute-start(f32[2,128]{1,0:T(2,128)S(1)} %get-tuple-element.21), channel_id=1, source_target_pairs={{0,10},{1,21},{2,8},{3,23},{4,14},{5,17},{6,12},{7,19},{8,2},{9,29... | collective-permute-start | bytes 3080 | tf_op jit(solution)/shard_map/ppermute | solution.py:233
  31.6 0.1 collective-permute-done.11
  31.7 1.6 %collective-permute-done.12 = f32[2,128]{1,0:T(2,128)S(1)} collective-permute-done((f32[2,128]{1,0:T(2,128)S(1)}, f32[2,128]{1,0:T(2,128)S(1)}, u32[]{:S(2)}, u32[]{:S(2)}) %collective-permute-start.12) | collective-permute-done | bytes 1056 | tf_op jit(solution)/shard_map/ppermute | solution.py:233
  33.3 1.4 %collective-permute-done.13 = f32[2,128]{1,0:T(2,128)S(1)} collective-permute-done((f32[2,128]{1,0:T(2,128)S(1)}, f32[2,128]{1,0:T(2,128)S(1)}, u32[]{:S(2)}, u32[]{:S(2)}) %collective-permute-start.13) | collective-permute-done | bytes 1056 | tf_op jit(solution)/shard_map/ppermute | solution.py:233
  34.8 1.4 %collective-permute-start.14 = (f32[1,128]{1,0:T(1,128)S(1)}, f32[1,128]{1,0:T(1,128)S(1)}, u32[]{:S(2)}, u32[]{:S(2)}) collective-permute-start(f32[1,128]{1,0:T(1,128)S(1)} %slice.23), channel_id=1, source_target_pairs={{0,1},{1,0},{2,3},{3,2},{4,5},{5,4},{6,7},{7,6},{8,9},{9,8},{10,11... | collective-permute-start | bytes 1544 | tf_op jit(solution)/shard_map/ppermute | solution.py:233
  36.1 0.8 %collective-permute-done.14 = f32[1,128]{1,0:T(1,128)S(1)} collective-permute-done((f32[1,128]{1,0:T(1,128)S(1)}, f32[1,128]{1,0:T(1,128)S(1)}, u32[]{:S(2)}, u32[]{:S(2)}) %collective-permute-start.14) | collective-permute-done | bytes 544 | tf_op jit(solution)/shard_map/ppermute | solution.py:233
  36.9 0.5 %fusion.4 = (f32[128]{0:T(128)}, f32[128]{0:T(128)}) fusion(f32[1,128]{1,0:T(1,128)S(1)} %collective-permute-done.14, pred[]{:T(512)S(6)} %eq.3, f32[2,128]{1,0:T(2,128)S(1)} %fusion.2), kind=kLoop, calls=%fused_computation.10 | loop fusion | flops 256 | bytes 2049 | tf_op jit(solution)/shard_map/reshape | solution.py:275
  (10 shorter events, 0.0 us)
Async XLA Ops:
  0.6 11.4 %collective-permute-start.1 = (bf16[128,768]{1,0:T(8,128)(2,1)}, bf16[128,768]{1,0:T(8,128)(2,1)S(1)}, u32[]{:S(2)}, u32[]{:S(2)}) collective-permute-start(bf16[128,768]{1,0:T(8,128)(2,1)} %image.1), channel_id=1, source_target_pairs={{0,8},{1,9},{2,10},{3,11},{4,12},{5,13},{6,14},{7,15},{8,0},{9,1},... | collective-permute-start | bytes 589832 | tf_op jit(solution)/shard_map/ppermute | solution.py:233
  3.7 10.3 %collective-permute-start.3 = (bf16[128,768]{1,0:T(8,128)(2,1)}, bf16[128,768]{1,0:T(8,128)(2,1)S(1)}, u32[]{:S(2)}, u32[]{:S(2)}) collective-permute-start(bf16[128,768]{1,0:T(8,128)(2,1)} %image.1), channel_id=1, source_target_pairs={{0,2},{1,3},{2,0},{3,1},{4,6},{5,7},{6,4},{7,5},{8,10},{9,11},{10,... | collective-permute-start | bytes 589832 | tf_op jit(solution)/shard_map/ppermute | solution.py:233
  5.3 11.6 %collective-permute-start.5 = (bf16[128,768]{1,0:T(8,128)(2,1)}, bf16[128,768]{1,0:T(8,128)(2,1)S(1)}, u32[]{:S(2)}, u32[]{:S(2)}) collective-permute-start(bf16[128,768]{1,0:T(8,128)(2,1)} %text.1), channel_id=1, source_target_pairs={{0,16},{1,17},{2,18},{3,19},{4,20},{5,21},{6,22},{7,23},{8,24},{9,... | collective-permute-start | bytes 589832 | tf_op jit(solution)/shard_map/ppermute | solution.py:233
  7.9 10.5 %collective-permute-start.7 = (bf16[128,768]{1,0:T(8,128)(2,1)}, bf16[128,768]{1,0:T(8,128)(2,1)S(1)}, u32[]{:S(2)}, u32[]{:S(2)}) collective-permute-start(bf16[128,768]{1,0:T(8,128)(2,1)} %image.1), channel_id=1, source_target_pairs={{0,10},{1,11},{2,8},{3,9},{4,14},{5,15},{6,12},{7,13},{8,2},{9,3},... | collective-permute-start | bytes 589832 | tf_op jit(solution)/shard_map/ppermute | solution.py:233
  8.2 10.2 %collective-permute-start = (bf16[128,768]{1,0:T(8,128)(2,1)}, bf16[128,768]{1,0:T(8,128)(2,1)S(1)}, u32[]{:S(2)}, u32[]{:S(2)}) collective-permute-start(bf16[128,768]{1,0:T(8,128)(2,1)} %image.1), channel_id=1, source_target_pairs={{0,1},{1,0},{2,3},{3,2},{4,5},{5,4},{6,7},{7,6},{8,9},{9,8},{10,11... | collective-permute-start | bytes 589832 | tf_op jit(solution)/shard_map/ppermute | solution.py:233
  12.1 11.2 %collective-permute-start.6 = (bf16[128,768]{1,0:T(8,128)(2,1)}, bf16[128,768]{1,0:T(8,128)(2,1)S(1)}, u32[]{:S(2)}, u32[]{:S(2)}) collective-permute-start(bf16[128,768]{1,0:T(8,128)(2,1)} %text.1), channel_id=1, source_target_pairs={{0,4},{1,5},{2,6},{3,7},{4,0},{5,1},{6,2},{7,3},{8,12},{9,13},{10,... | collective-permute-start | bytes 589832 | tf_op jit(solution)/shard_map/ppermute | solution.py:233
  14.1 9.2 %collective-permute-start.2 = (bf16[128,768]{1,0:T(8,128)(2,1)S(1)}, bf16[128,768]{1,0:T(8,128)(2,1)S(1)}, u32[]{:S(2)}, u32[]{:S(2)}) collective-permute-start(bf16[128,768]{1,0:T(8,128)(2,1)S(1)} %collective-permute-done.1.refs_4_), channel_id=1, source_target_pairs={{0,1},{1,0},{2,3},{3,2},{4,5},{5,4},{6,7},{7,6},{8,9},{9,8},{10,11... | collective-permute-start | bytes 589832 | tf_op jit(solution)/shard_map/ppermute | solution.py:233
  16.8 6.5 %collective-permute-start.4 = (bf16[128,768]{1,0:T(8,128)(2,1)S(1)}, bf16[128,768]{1,0:T(8,128)(2,1)S(1)}, u32[]{:S(2)}, u32[]{:S(2)}) collective-permute-start(bf16[128,768]{1,0:T(8,128)(2,1)S(1)} %collective-permute-done.3.refs_6_), channel_id=1, source_target_pairs={{0,1},{1,0},{2,3},{3,2},{4,5},{5,4},{6,7},{7,6},{8,9},{9,8},{10,11... | collective-permute-start | bytes 589832 | tf_op jit(solution)/shard_map/ppermute | solution.py:233
  18.4 6.4 %collective-permute-start.8 = (bf16[128,768]{1,0:T(8,128)(2,1)S(1)}, bf16[128,768]{1,0:T(8,128)(2,1)S(1)}, u32[]{:S(2)}, u32[]{:S(2)}) collective-permute-start(bf16[128,768]{1,0:T(8,128)(2,1)S(1)} %collective-permute-done.7.refs_6_), channel_id=1, source_target_pairs={{0,1},{1,0},{2,3},{3,2},{4,5},{5,4},{6,7},{7,6},{8,9},{9,8},{10,11... | collective-permute-start | bytes 589832 | tf_op jit(solution)/shard_map/ppermute | solution.py:233
  18.4 7.3 %collective-permute-start.9 = (bf16[128,768]{1,0:T(8,128)(2,1)S(1)}, bf16[128,768]{1,0:T(8,128)(2,1)S(1)}, u32[]{:S(2)}, u32[]{:S(2)}) collective-permute-start(bf16[128,768]{1,0:T(8,128)(2,1)S(1)} %collective-permute-done.5.refs_8_), channel_id=1, source_target_pairs={{0,4},{1,5},{2,6},{3,7},{4,0},{5,1},{6,2},{7,3},{8,12},{9,13},{10,... | collective-permute-start | bytes 589832 | tf_op jit(solution)/shard_map/ppermute | solution.py:233
  21.2 0.9 %copy-start = (bf16[128,768]{1,0:T(8,128)(2,1)S(1)}, bf16[128,768]{1,0:T(8,128)(2,1)}, u32[]{:S(2)}) copy-start(bf16[128,768]{1,0:T(8,128)(2,1)} %image.1) | copy-start | bytes 589828
  22.1 0.9 %copy-start.1 = (bf16[128,768]{1,0:T(8,128)(2,1)S(1)}, bf16[128,768]{1,0:T(8,128)(2,1)}, u32[]{:S(2)}) copy-start(bf16[128,768]{1,0:T(8,128)(2,1)} %text.1) | copy-start | bytes 589828
  26.8 1.2 %collective-permute-start.10 = (f32[4,2,128]{2,1,0:T(2,128)S(1)}, f32[4,2,128]{2,1,0:T(2,128)S(1)}, u32[]{:S(2)}, u32[]{:S(2)}) collective-permute-start(f32[4,2,128]{2,1,0:T(2,128)S(1)} %get-tuple-element.19), channel_id=1, source_target_pairs={{0,1},{1,0},{2,3},{3,2},{4,5},{5,4},{6,7},{7,6},{8,9},{9,8},{10,11... | collective-permute-start | bytes 12296 | tf_op jit(solution)/shard_map/ppermute | solution.py:233
  28.1 3.6 %collective-permute-start.11 = (f32[2,128]{1,0:T(2,128)S(1)}, f32[2,128]{1,0:T(2,128)S(1)}, u32[]{:S(2)}, u32[]{:S(2)}) collective-permute-start(f32[2,128]{1,0:T(2,128)S(1)} %get-tuple-element.20), channel_id=1, source_target_pairs={{0,8},{1,17},{2,10},{3,19},{4,12},{5,21},{6,14},{7,23},{8,0},{9,25... | collective-permute-start | bytes 3080 | tf_op jit(solution)/shard_map/ppermute | solution.py:233
  29.8 3.6 %collective-permute-start.12 = (f32[2,128]{1,0:T(2,128)S(1)}, f32[2,128]{1,0:T(2,128)S(1)}, u32[]{:S(2)}, u32[]{:S(2)}) collective-permute-start(f32[2,128]{1,0:T(2,128)S(1)} %get-tuple-element.22), channel_id=1, source_target_pairs={{0,2},{1,5},{2,0},{3,7},{4,6},{5,1},{6,4},{7,3},{8,10},{9,13},{10,... | collective-permute-start | bytes 3080 | tf_op jit(solution)/shard_map/ppermute | solution.py:233
  30.3 4.5 %collective-permute-start.13 = (f32[2,128]{1,0:T(2,128)S(1)}, f32[2,128]{1,0:T(2,128)S(1)}, u32[]{:S(2)}, u32[]{:S(2)}) collective-permute-start(f32[2,128]{1,0:T(2,128)S(1)} %get-tuple-element.21), channel_id=1, source_target_pairs={{0,10},{1,21},{2,8},{3,23},{4,14},{5,17},{6,12},{7,19},{8,2},{9,29... | collective-permute-start | bytes 3080 | tf_op jit(solution)/shard_map/ppermute | solution.py:233
  34.8 2.2 %collective-permute-start.14 = (f32[1,128]{1,0:T(1,128)S(1)}, f32[1,128]{1,0:T(1,128)S(1)}, u32[]{:S(2)}, u32[]{:S(2)}) collective-permute-start(f32[1,128]{1,0:T(1,128)S(1)} %slice.23), channel_id=1, source_target_pairs={{0,1},{1,0},{2,3},{3,2},{4,5},{5,4},{6,7},{7,6},{8,9},{9,8},{10,11... | collective-permute-start | bytes 1544 | tf_op jit(solution)/shard_map/ppermute | solution.py:233
